TPU v7x, 32 devices: a whole 2x2x4 slice. The times are simulated.
32 devices in a mesh: rep: 1, dp: 32 (over x, y, z, core).
Axes of the slice: x: 2, y: 2, z: 4, core: 2. Of those that a mesh axis runs over, the one named last changes fastest.
Arguments:
- x: bfloat16 [32, 2048, 768], P(('rep', 'dp'))
- dy: bfloat16 [32, 2048, 768], P(('rep', 'dp'))
- w_gate: bfloat16 [2, 768, 1792], P(None, 'dp')
- w_up: bfloat16 [2, 768, 1792], P(None, 'dp')
- w_down: bfloat16 [2, 1792, 768], P(None, 'dp')
Outputs:
- output 1: bfloat16 [32, 2048, 768], P(('rep', 'dp'))
- output 2: bfloat16 [2, 768, 1792], P('rep', 'dp')
- output 3: bfloat16 [2, 768, 1792], P('rep', 'dp')
- output 4: bfloat16 [2, 1792, 768], P('rep', 'dp')
All inputs are finite; a program needn't handle non-finite values.
Results may differ from a plain program's by a relative error of at most 0.018.
Values are sent between devices in bfloat16 or wider.
A program may use at most 2 GiB of HBM per device.

v0:
```python
import jax
import jax.numpy as jnp
from jax import lax

NAMES = ("w_gate", "w_up", "w_down")


def matmul(a, w):
    return jnp.dot(a, w, preferred_element_type=jnp.float32).astype(jnp.bfloat16)


def normed(h):
    wide = h.astype(jnp.float32)
    scale = lax.rsqrt(jnp.mean(wide**2, -1, keepdims=True) + 1e-6)
    return (wide * scale).astype(jnp.bfloat16)


def layer(h, w):
    a = normed(h)
    gate = jnp.dot(a, w["w_gate"], preferred_element_type=jnp.float32)
    up = jnp.dot(a, w["w_up"], preferred_element_type=jnp.float32)
    return h + matmul((jax.nn.silu(gate) * up).astype(jnp.bfloat16), w["w_down"])


def stack(weights, h):
    for number in range(weights["w_gate"].shape[0]):
        h = layer(h, {name: w[number] for name, w in weights.items()})
    return h


def solution(mesh):
    groups = mesh.shape["rep"]

    def step(x, dy, *weights):
        shape = x.shape
        x, dy = (t.reshape(groups, -1, *t.shape[1:]) for t in (x, dy))

        def of_a_group(x, dy):
            _, back = jax.vjp(stack, dict(zip(NAMES, weights, strict=True)), x)
            by_weights, by_x = back(dy)
            return (by_x, *(by_weights[name] for name in NAMES))

        by_x, *by_weights = jax.vmap(of_a_group)(x, dy)
        return (by_x.reshape(shape), *(t.reshape(-1, *t.shape[2:]) for t in by_weights))

    return step
```

profile of v0, /device:TPU:0, one launch (start us, length us, event | category | flops | bytes accessed | tf_op | source)
XLA Modules:
  0.0 1639.4 jit_solution(14648255917750570874)
XLA Ops:
  32.8 183.6 %while.13 = (bf16[1,2048,768]{2,1,0:T(8,128)(2,1)S(1)}, bf16[1,56,768]{2,1,0:T(8,128)(2,1)S(1)}, bf16[1,2048,1792]{1,2,0:T(8,128)(2,1)}, bf16[1,56,768]{2,1,0:T(...) while((bf16[1,2048,768]{2,1,0:T(8,128)(2,1)S(1)}, ...), condition=%wide.windowed_dot_general_cond_ag, body=%wide.windowed_dot_general_body_ag.sunk | while | flops 704815104 | bytes 10764829 | solution.py:9
  32.8 6.4 collective-permute-start
  55.5 5.4 collective-permute-done.3
  77.2 5.4 collective-permute-done.3
  98.9 5.4 collective-permute-done.3
  121.1 6.6 collective-permute-done.3
  144.0 5.4 collective-permute-done.3
  165.7 5.9 collective-permute-done.3
  188.3 5.8 collective-permute-done.3
  210.5 6.0 collective-permute-done.3
  216.4 10.0 copy.2
  226.5 11.4 fusion.216
  237.9 16.3 fusion.176
  254.2 10.7 copy.6
  264.9 9.9 fusion.189
  279.2 11.3 fusion.212
  290.5 25.8 %all-gather.35.cloned.1.call-done = bf16[1,768,1792]{2,1,0:T(8,128)(2,1)} async-done(((bf16[1,24,1792]{2,1,0:T(8,128)(2,1)}), bf16[1,768,1792]{2,1,0:T(8,128)(2,1)}) %all-gather.35.cloned.1.call-update) | async-done | bytes 2752528 | tf_op jit(solution)/vmap(jvp())/squeeze | solution.py:27
  316.3 16.4 %fusion.170 = (bf16[1,2048,1792]{2,1,0:T(8,128)(2,1)}, f32[2048,1792]{1,0:T(8,128)}) fusion(f32[2048,1792]{1,0:T(8,128)} %fusion.212, bf16[1,768,1792]{2,1,0:T(8,128)(2,1)} %all-gather.35.cloned.1.call-done, bf16[1,2048,768]{1,2,0:T(8,128)(2,1)} %fusion.190), kind=kOutput, calls=%fused_computation.205 | convolution fusion | flops 5659164672 | bytes 42598400 | tf_op jit(solution)/vmap(jvp())/dot_general | solution.py:21
  332.7 10.3 copy.4
  343.0 181.9 %while.18 = (bf16[1,2048,1792]{1,2,0:T(8,128)(2,1)}, bf16[1,2048,768]{2,1,0:T(8,128)(2,1)S(1)}, f32[56,768]{1,0:T(8,128)S(1)}, f32[56,768]{1,0:T(8,128)}, u32[]{...) while((bf16[1,2048,1792]{1,2,0:T(8,128)(2,1)}, ...), condition=%wide.windowed_dot_general_cond_rs.4.clone, body=%wide.windowed_dot_general_body_rs.4.clone.sunk | while | flops 706736128 | bytes 27165264 | solution.py:9
  524.9 14.0 fusion.161
  539.0 6.1 fusion.195
  545.9 6.4 fusion.191
  558.0 179.1 %while.19 = (bf16[1,2048,768]{2,1,0:T(8,128)(2,1)}, bf16[1,2048,1792]{1,2,0:T(8,128)(2,1)}, f32[768,56]{0,1:T(8,128)S(1)}, f32[768,56]{0,1:T(8,128)}, u32[]{:T(1...) while((bf16[1,2048,768]{2,1,0:T(8,128)(2,1)}, ...), condition=%wide.windowed_dot_general_cond_rs.5.clone, body=%wide.windowed_dot_general_body_rs.5.clone.sunk | while | flops 706736128 | bytes 69108360 | solution.py:9
  569.3 5.4 collective-permute-start.27
  591.8 5.4 collective-permute-start.27
  614.3 5.4 collective-permute-start.27
  636.8 5.4 collective-permute-start.27
  659.3 5.4 collective-permute-start.27
  681.8 5.4 collective-permute-start.27
  704.3 5.4 collective-permute-start.27
  726.8 5.4 collective-permute-start.27
  737.8 209.1 %while.16 = (bf16[1,2048,1792]{2,1,0:T(8,128)(2,1)}, bf16[1,2048,768]{1,2,0:T(8,128)(2,1)S(1)}, f32[1792,24]{0,1:T(8,128)}, f32[1792,24]{0,1:T(8,128)}, u32[]{:T...) while((bf16[1,2048,1792]{2,1,0:T(8,128)(2,1)}, ...), condition=%wide.windowed_dot_general_cond_rs.2.clone, body=%wide.windowed_dot_general_body_rs.2.clone.sunk | while | flops 705687552 | bytes 27165264 | solution.py:21
  750.9 5.3 collective-permute-start.15
  777.2 5.3 collective-permute-start.15
  803.6 5.3 collective-permute-start.15
  829.9 5.3 collective-permute-start.15
  856.3 5.3 collective-permute-start.15
  882.6 5.3 collective-permute-start.15
  909.0 5.3 collective-permute-start.15
  935.3 5.3 collective-permute-start.15
  946.9 23.8 %fusion.163 = (bf16[1,2048,1792]{2,1,0:T(8,128)(2,1)}, bf16[1,2048,1792]{2,1,0:T(8,128)(2,1)}) fusion(f32[2048,1792]{1,0:T(8,128)} %fusion.216, f32[2048,1792]{1,0:T(8,128)} %get-tuple-element.282, bf16[1,1792,768]{2,1,0:T(8,128)(2,1)} %all-gather.31.cloned.1.call-done, bf16[1,2048,768]{1,2,0:T(8,128)(2,1)} %copy-done.8), kind=kOutput, calls=%fused_computation.197 | convolution fusion | flops 5695864832 | bytes 49938432 | tf_op jit(solution)/vmap(transpose(jvp()))/dot_general | solution.py:9
  970.7 209.0 %while.17 = (bf16[1,2048,1792]{2,1,0:T(8,128)(2,1)}, bf16[1,2048,768]{1,2,0:T(8,128)(2,1)S(1)}, f32[1792,24]{0,1:T(8,128)}, f32[1792,24]{0,1:T(8,128)}, u32[]{:T...) while((bf16[1,2048,1792]{2,1,0:T(8,128)(2,1)}, ...), condition=%wide.windowed_dot_general_cond_rs.3.clone, body=%wide.windowed_dot_general_body_rs.3.clone.sunk | while | flops 705687552 | bytes 27165264 | solution.py:21
  983.7 5.3 collective-permute-start.19
  1010.0 5.3 collective-permute-start.19
  1036.4 5.3 collective-permute-start.19
  1062.7 5.3 collective-permute-start.19
  1089.1 5.3 collective-permute-start.19
  1115.4 5.3 collective-permute-start.19
  1141.8 5.3 collective-permute-start.19
  1168.1 5.3 collective-permute-start.19
  1179.7 211.8 %while.14 = (bf16[1,2048,1792]{2,1,0:T(8,128)(2,1)}, bf16[1,2048,768]{1,2,0:T(8,128)(2,1)}, f32[1792,24]{0,1:T(8,128)}, f32[1792,24]{0,1:T(8,128)}, u32[]{:T(128...) while((bf16[1,2048,1792]{2,1,0:T(8,128)(2,1)}, ...), condition=%wide.windowed_dot_general_cond_rs.clone, body=%wide.windowed_dot_general_body_rs.clone.sunk | while | flops 705687552 | bytes 27165264 | solution.py:20
  1192.8 5.3 collective-permute-start.7
  1219.5 5.3 collective-permute-start.7
  1246.2 5.3 collective-permute-start.7
  1326.3 5.3 collective-permute-start.7
  1353.0 5.3 collective-permute-start.7
  1379.7 5.3 collective-permute-start.7
  1391.5 208.9 %while.15 = (bf16[1,2048,1792]{2,1,0:T(8,128)(2,1)}, bf16[1,2048,768]{1,2,0:T(8,128)(2,1)S(1)}, f32[1792,24]{0,1:T(8,128)}, f32[1792,24]{0,1:T(8,128)}, u32[]{:T...) while((bf16[1,2048,1792]{2,1,0:T(8,128)(2,1)}, ...), condition=%wide.windowed_dot_general_cond_rs.1.clone, body=%wide.windowed_dot_general_body_rs.1.clone.sunk | while | flops 705687552 | bytes 27165264 | solution.py:20
  1431.0 5.3 collective-permute-start.11
  1457.3 5.3 collective-permute-start.11
  1562.6 5.3 collective-permute-start.11
  1600.6 9.1 fusion.201
  1609.8 6.4 fusion.188
  (893 shorter events, 1204.7 us)
Async XLA Ops:
  7.2 219.3 %all-gather.27.cloned.1.call-start = ((), (), s32[]{:S(2)}) async-start(), calls=%async_computation | async-start | bytes 2838528 | tf_op jit(solution)/vmap(jvp())/squeeze | solution.py:27
  8.9 229.0 %all-gather.29.cloned.1.call-start = ((), (), s32[]{:S(2)}) async-start(), calls=%async_computation.1 | async-start | bytes 2838528 | tf_op jit(solution)/vmap(jvp())/squeeze | solution.py:27
  10.5 254.4 %all-gather.31.cloned.1.call-start = ((), (), s32[]{:S(2)}) async-start(), calls=%async_computation.2 | async-start | bytes 2838528 | tf_op jit(solution)/vmap(jvp())/squeeze | solution.py:27
  12.2 267.0 %all-gather.33.cloned.1.call-start = ((), (), s32[]{:S(2)}) async-start(), calls=%async_computation.3 | async-start | bytes 2838528 | tf_op jit(solution)/vmap(jvp())/squeeze | solution.py:27
  12.8 303.5 %all-gather.35.cloned.1.call-start = ((), (), s32[]{:S(2)}) async-start(), calls=%async_computation.4 | async-start | bytes 2838528 | tf_op jit(solution)/vmap(jvp())/squeeze | solution.py:27
  12.8 16.1 collective-permute-start.28
  32.8 12.5 collective-permute-start
  366.2 10.2 collective-permute-start.20
  389.0 10.2 collective-permute-start.20
  411.8 10.2 collective-permute-start.20
  434.6 10.2 collective-permute-start.20
  457.4 10.2 collective-permute-start.20
  480.2 10.2 collective-permute-start.20
  503.0 10.2 collective-permute-start.20
  524.9 1098.6 %collective-permute-start.33 = (f32[56,768]{1,0:T(8,128)}, f32[56,768]{1,0:T(8,128)}, u32[]{:S(2)}, u32[]{:S(2)}) collective-permute-start(f32[56,768]{1,0:T(8,128)} %get-tuple-element.52), channel_id=46, source_target_pairs={{0,1},{1,2},{2,3},{3,4},{4,5},{5,6},{6,7},{7,8},{8,9},{9,10},{10,1... | collective-permute-start | bytes 516104 | tf_op jit(solution)/vmap(transpose(jvp()))/dot_general | solution.py:9
  580.5 10.1 collective-permute-start.24
  603.0 10.1 collective-permute-start.24
  625.5 10.1 collective-permute-start.24
  648.0 10.1 collective-permute-start.24
  670.5 10.1 collective-permute-start.24
  693.0 10.1 collective-permute-start.24
  715.5 10.1 collective-permute-start.24
  737.1 887.5 %collective-permute-start.34 = (f32[768,56]{0,1:T(8,128)}, f32[768,56]{0,1:T(8,128)}, u32[]{:S(2)}, u32[]{:S(2)}) collective-permute-start(f32[768,56]{0,1:T(8,128)} %get-tuple-element.54), channel_id=52, source_target_pairs={{0,1},{1,2},{2,3},{3,4},{4,5},{5,6},{6,7},{7,8},{8,9},{9,10},{10,1... | collective-permute-start | bytes 516104 | tf_op jit(solution)/vmap(transpose(jvp()))/dot_general | solution.py:9
  738.6 10.5 collective-permute-start.12
  764.1 11.4 collective-permute-start.12
  790.4 11.4 collective-permute-start.12
  816.7 11.4 collective-permute-start.12
  843.1 11.4 collective-permute-start.12
  869.4 11.4 collective-permute-start.12
  895.8 11.4 collective-permute-start.12
  922.1 11.4 collective-permute-start.12
  946.9 674.5 %collective-permute-start.31 = (f32[1792,24]{0,1:T(8,128)}, f32[1792,24]{0,1:T(8,128)}, u32[]{:S(2)}, u32[]{:S(2)}) collective-permute-start(f32[1792,24]{0,1:T(8,128)} %get-tuple-element.48), channel_id=34, source_target_pairs={{0,1},{1,2},{2,3},{3,4},{4,5},{5,6},{6,7},{7,8},{8,9},{9,10},{10,1... | collective-permute-start | bytes 516104 | tf_op jit(solution)/vmap(transpose(jvp()))/dot_general | solution.py:21
  971.4 10.5 collective-permute-start.16
  996.9 11.4 collective-permute-start.16
  1023.2 11.4 collective-permute-start.16
  1049.6 11.4 collective-permute-start.16
  1075.9 11.4 collective-permute-start.16
  1102.3 11.4 collective-permute-start.16
  1128.6 11.4 collective-permute-start.16
  1155.0 11.4 collective-permute-start.16
  1180.4 10.6 collective-permute-start.4
  1206.2 11.5 collective-permute-start.4
  1219.5 10.1 collective-permute-start.6
  1219.5 10.1 collective-permute-start.7
  1232.9 11.5 collective-permute-start.4
  1259.6 11.5 collective-permute-start.4
  1286.3 11.5 collective-permute-start.4
  1313.0 11.5 collective-permute-start.4
  1326.3 10.1 collective-permute-start.6
  1326.3 10.1 collective-permute-start.7
  1339.7 11.5 collective-permute-start.4
  1366.4 11.5 collective-permute-start.4
  1379.7 10.1 collective-permute-start.6
  1379.7 10.1 collective-permute-start.7
  1392.4 10.5 collective-permute-start.8
  1417.8 11.4 collective-permute-start.8
  1444.2 11.4 collective-permute-start.8
  1470.5 11.4 collective-permute-start.8
  1496.8 11.4 collective-permute-start.8
  1523.1 11.4 collective-permute-start.8
  1549.4 11.4 collective-permute-start.8
  1575.8 11.4 collective-permute-start.8
  1600.5 22.0 %collective-permute-start.32 = (f32[1792,24]{0,1:T(8,128)}, f32[1792,24]{0,1:T(8,128)}, u32[]{:S(2)}, u32[]{:S(2)}) collective-permute-start(f32[1792,24]{0,1:T(8,128)} %get-tuple-element.50), channel_id=40, source_target_pairs={{0,1},{1,2},{2,3},{3,4},{4,5},{5,6},{6,7},{7,8},{8,9},{9,10},{10,1... | collective-permute-start | bytes 516104 | tf_op jit(solution)/vmap(transpose(jvp()))/dot_general | solution.py:21
  1621.4 10.3 collective-permute-start.30
  (213 other events, 2127.8 us)
Sparse Core Ops, SparseCore 0:
  11.0 62.1 all-gather.26
  76.3 58.6 all-gather.28
  138.0 58.0 all-gather.30
  198.9 57.4 all-gather.32
  259.3 56.9 all-gather.34
where the time goes:
time: 1660 us; the launch traced here: 1640 us
  starting transfers between devices  554 us (33%)
  matrix products  495 us (30%)
  other arithmetic  294 us (18%)
  waiting for transfers between devices  183 us (11%)
  local copies, waits for them, and re-layouts  95.3 us (6%)
    dot_general x99, starting transfers between devices, matmul(): jnp.dot(a, w, preferred_element_type=jnp.float32).astype(jnp.bfloat16)  212 us
    dot_general x36, matrix products, layer(): up = jnp.dot(a, w['w_up'], preferred_element_type=jnp.float32)  189 us
    dot_general x36, matrix products, layer(): gate = jnp.dot(a, w['w_gate'], preferred_element_type=jnp.float32)  179 us
    dot_general x66, starting transfers between devices, layer(): up = jnp.dot(a, w['w_up'], preferred_element_type=jnp.float32)  171 us
    dot_general x66, starting transfers between devices, layer(): gate = jnp.dot(a, w['w_gate'], preferred_element_type=jnp.float32)  171 us
    dot_general x99, waiting for transfers between devices, matmul(): jnp.dot(a, w, preferred_element_type=jnp.float32).astype(jnp.bfloat16)  150 us
    dot_general x50, matrix products, matmul(): jnp.dot(a, w, preferred_element_type=jnp.float32).astype(jnp.bfloat16)  126 us
    dot_general x96, other arithmetic  119 us
  transfers between devices with their start and end apart: 236, of which 74 were waited for; matrix products, arithmetic and copies ran while one was open for 51% of the time, Pallas kernels for 0%

commit v1 on v0

v1 whole, which is shorter than its diff:
```python
import functools
import jax
import jax.numpy as jnp
from jax import lax
from jax.experimental import pallas as pl
from jax.experimental.pallas import tpu as pltpu
from jax.sharding import PartitionSpec as P

F32 = jnp.float32
BF16 = jnp.bfloat16
LAYERS, TOKENS, D, FF = 2, 2048, 768, 1792
GRID = (2, 2, 4, 2)
GU_UNITS = {"A": (0, 1), "B": (1, 1), "C": (2, 1)}
DN_UNITS = {"A": (0, 2), "B": (2, 3), "C": (5, 2)}
ALL = slice(None)


def place():
    me = lax.axis_index("dp")
    c = lax.rem(me, 2)
    z = lax.rem(me // 2, 4)
    y = lax.rem(me // 8, 2)
    x = me // 16
    return x, y, z, c


def index(x, y, z, c):
    return ((x * 2 + y) * 4 + z) * 2 + c


def after(z):
    return lax.rem(2 * z + 1, 5)


def before(z):
    return lax.rem(3 * z + 2, 5)


def greet():
    x, y, z, c = place()
    barrier = pltpu.get_barrier_semaphore()
    for other in (index(x, y, z, 1 - c), index(1 - x, y, z, c), index(x, 1 - y, z, c), index(x, y, after(z), c), index(x, y, before(z), c)):
        pl.semaphore_signal(barrier, inc=1, device_id={"dp": other}, device_id_type=pl.DeviceIdType.MESH)
    pl.semaphore_wait(barrier, 5)


class Copies:
    def __init__(self, send, recv):
        self.send, self.recv, self.made, self.used = send, recv, {}, 0

    def start(self, name, pairs, to):
        made = []
        for src, dst in pairs:
            copy = pltpu.make_async_remote_copy(src_ref=src, dst_ref=dst, send_sem=self.send.at[self.used], recv_sem=self.recv.at[self.used],
                                                device_id={"dp": to}, device_id_type=pl.DeviceIdType.MESH)
            copy.start()
            made.append(copy)
            self.used += 1
        assert name not in self.made
        self.made[name] = made

    def wait(self, name):
        for copy in self.made[name]:
            copy.wait_recv()

    def finish(self):
        for made in self.made.values():
            for copy in made:
                copy.wait_send()


GATHER_COPIES = 160


def gather_steps(copies, gu_in, dn_in, gu, dn, gs, ds, tag):
    x, y, z, c = place()
    X, Y = 1 - x, 1 - y
    ring = [z]
    for _ in range(3):
        ring.append(before(ring[-1]))
    to = {"x": index(X, y, z, c), "y": index(x, Y, z, c), "z": index(x, y, after(z), c), "c": index(x, y, z, 1 - c)}

    def region(colour, xs, ys, k):
        a, n = GU_UNITS[colour]
        b, m = DN_UNITS[colour]
        return (gu.at[gs, xs, ys, ring[k], c, pl.ds(a, n)], dn.at[ds, xs, ys, ring[k], c, pl.ds(b, m)])

    def own(colour):
        a, n = GU_UNITS[colour]
        b, m = DN_UNITS[colour]
        return (gu_in.at[gs, pl.ds(a, n)], dn_in.at[ds, pl.ds(b, m)])

    def send(name, way, colour, xs, ys, k, mine=False):
        dst = region(colour, xs, ys, k)
        src = own(colour) if mine else dst
        copies.start(tag + colour + name, tuple(zip(src, dst)), to[way])

    def arrived(name, colour, xs, ys, k):
        copies.wait(tag + colour + name)

    def share(name, colour, xs, ys, k):
        reg = region(colour, xs, ys, k)
        copies.start(tag + colour + name + "s", tuple(zip(reg, reg)), to["c"])
        shared.append((tag + colour + name + "s"))

    shared = []
    send("x", "x", "C", x, y, 0, True)
    send("y", "y", "B", x, y, 0, True)
    send("z1", "z", "A", x, y, 0, True)
    send("x0", "x", "A", x, y, 0, True)
    send("y0", "y", "A", x, y, 0, True)
    full = (gu.at[gs, x, y, z, c], dn.at[ds, x, y, z, c])
    copies.start(tag + "own", tuple(zip((gu_in.at[gs], dn_in.at[ds]), full)), to["c"])
    shared.append(tag + "own")
    yield
    yield
    copies.wait(tag + "Cx")
    send("z1", "z", "C", ALL, y, 0)
    send("y0", "y", "C", ALL, y, 0)
    share("x", "C", X, y, 0)
    yield
    copies.wait(tag + "By")
    send("z1", "z", "B", x, ALL, 0)
    send("x0", "x", "B", x, ALL, 0)
    share("y", "B", x, Y, 0)
    for k in (1, 2, 3):
        yield
        copies.wait(tag + f"Az{k}")
        if k < 3:
            send(f"z{k + 1}", "z", "A", x, y, k)
        send(f"x{k}", "x", "A", x, y, k)
        send(f"y{k}", "y", "A", x, y, k)
        share(f"z{k}", "A", x, y, k)
        yield
        copies.wait(tag + f"Ax{k - 1}")
        send(f"Y{k - 1}", "y", "A", X, y, k - 1)
        share(f"x{k - 1}", "A", X, y, k - 1)
        yield
        copies.wait(tag + f"Cz{k}")
        if k < 3:
            send(f"z{k + 1}", "z", "C", ALL, y, k)
        send(f"y{k}", "y", "C", ALL, y, k)
        share(f"z{k}", "C", ALL, y, k)
        yield
        copies.wait(tag + f"Bz{k}")
        if k < 3:
            send(f"z{k + 1}", "z", "B", x, ALL, k)
        send(f"x{k}", "x", "B", x, ALL, k)
        share(f"z{k}", "B", x, ALL, k)
    yield
    copies.wait(tag + "Ax3")
    send("Y3", "y", "A", X, y, 3)
    share("x3", "A", X, y, 3)
    for k in range(4):
        yield
        copies.wait(tag + f"Bx{k}")
        share(f"x{k}", "B", X, ALL, k)
        yield
        copies.wait(tag + f"Cy{k}")
        share(f"y{k}", "C", ALL, Y, k)
        yield
        copies.wait(tag + f"Ay{k}")
        copies.wait(tag + f"AY{k}")
        share(f"y{k}", "A", ALL, Y, k)
    for name in shared:
        yield
        copies.wait(name)


def gather_kernel(gu_in, dn_in, gu, dn, gu_own, dn_own, send, recv, local):
    x, y, z, c = place()
    greet()
    copies = Copies(send, recv)
    steps = gather_steps(copies, gu_in, dn_in, gu, dn, ALL, ALL, "")
    next(steps)
    one = pltpu.make_async_copy(gu_in, gu_own, local.at[0])
    two = pltpu.make_async_copy(dn_in, dn_own, local.at[1])
    one.start()
    two.start()
    one.wait()
    two.wait()
    one = pltpu.make_async_copy(gu_own, gu.at[ALL, x, y, z, c], local.at[2])
    two = pltpu.make_async_copy(dn_own, dn.at[ALL, x, y, z, c], local.at[3])
    one.start()
    two.start()
    one.wait()
    two.wait()
    for _ in steps:
        pass
    copies.finish()


def gather(gu_in, dn_in):
    hbm = pl.BlockSpec(memory_space=pl.ANY)
    return pl.pallas_call(
        gather_kernel, name="gather",
        out_shape=(jax.ShapeDtypeStruct((4, *GRID, 3, 8, FF), BF16), jax.ShapeDtypeStruct((2, *GRID, 7, 8, D), BF16)),
        in_specs=[hbm, hbm], out_specs=(hbm, hbm),
        scratch_shapes=[pltpu.VMEM((4, 3, 8, FF), BF16), pltpu.VMEM((2, 7, 8, D), BF16),
                        pltpu.SemaphoreType.DMA((GATHER_COPIES,)), pltpu.SemaphoreType.DMA((GATHER_COPIES,)), pltpu.SemaphoreType.DMA((4,))],
        compiler_params=pltpu.CompilerParams(collective_id=0, has_side_effects=True),
    )(gu_in, dn_in)


SCATTER_COPIES = 700
ROOM = 15


def add_pairs(dst, src, count, pairs):
    def body(m, _):
        for i, j in pairs:
            dst[(m, *i)] = (dst[(m, *i)].astype(F32) + src[(m, *j)].astype(F32)).astype(BF16)
        return 0
    lax.fori_loop(0, count, body, 0)


def scatter_steps(copies, gus, dns, gu, dn, sgu, sdn, arrive, tag):
    x, y, z, c = place()
    X, Y = 1 - x, 1 - y
    ring = [z]
    for _ in range(3):
        ring.append(before(ring[-1]))
    to = {"x": index(X, y, z, c), "y": index(x, Y, z, c), "z": index(x, y, after(z), c), "c": index(x, y, z, 1 - c)}
    M, N = len(gus), len(dns)
    slots, used = {}, {"A": 0, "B": 0, "C": 0}

    def half(colour, far):
        if colour == "B":
            return (X if far else x), ALL
        return ALL, (Y if far else y)

    def blocks(xs, ys):
        return [(e, ys) for e in range(2)] if xs is ALL else [(xs, e) for e in range(2)] if ys is ALL else [(xs, ys)]

    def swap(k, far):
        for colour in "ACB":
            xs, ys = half(colour, far)
            (a, n), (b, m) = GU_UNITS[colour], DN_UNITS[colour]
            pairs = [(gus[i].at[xs, ys, ring[k], 1 - c, pl.ds(a, n)], sgu.at[i, xs, ys, ring[k], pl.ds(a, n)]) for i in range(M)]
            pairs += [(dns[i].at[xs, ys, ring[k], 1 - c, pl.ds(b, m)], sdn.at[i, xs, ys, ring[k], pl.ds(b, m)]) for i in range(N)]
            copies.start(f"{tag}s{colour}{k}{far}", pairs, to["c"])

    def swapped(k, far):
        for colour in "ACB":
            copies.wait(f"{tag}s{colour}{k}{far}")
            here = blocks(*half(colour, far))
            for buf, other, count, (a, n) in ((gu, sgu, M, GU_UNITS[colour]), (dn, sdn, N, DN_UNITS[colour])):
                at = [(bx, by, ring[k], a + u) for bx, by in here for u in range(n)]
                add_pairs(buf, other, count, [(i, i) for i in at])

    def send(name, way, colour, xs, ys, k):
        (a, n), (b, m) = GU_UNITS[colour], DN_UNITS[colour]
        number = len(blocks(xs, ys))
        at = used[colour]
        used[colour] += number
        slots[colour + name] = at
        to_at = pl.ds(at, number) if number == 2 else at
        rgu, rdn = arrive[colour]
        copies.start(tag + colour + name, [(gu.at[ALL, xs, ys, ring[k], pl.ds(a, n)], rgu.at[ALL, to_at]),
                                           (dn.at[ALL, xs, ys, ring[k], pl.ds(b, m)], rdn.at[ALL, to_at])], to[way])

    def take(name, colour, xs, ys, k):
        copies.wait(tag + colour + name)
        at = slots[colour + name]
        for buf, other, count, (a, n) in ((gu, arrive[colour][0], M, GU_UNITS[colour]), (dn, arrive[colour][1], N, DN_UNITS[colour])):
            pairs = [((bx, by, ring[k], a + u), (at + e, u)) for e, (bx, by) in enumerate(blocks(xs, ys)) for u in range(n)]
            add_pairs(buf, other, count, pairs)

    def far(k):
        swapped(k, True)
        send(f"y{k}", "y", "A", ALL, Y, k)
        send(f"y{k}", "y", "C", ALL, Y, k)
        send(f"x{k}", "x", "B", X, ALL, k)

    def second(k):
        t = k or 4
        take(f"y{k}", "A", ALL, y, k)
        send(f"x{k}", "x", "A", X, y, k)
        yield
        take(f"y{k}", "C", ALL, y, k)
        if t > 1:
            take(f"z{t - 1}", "C", ALL, y, k)
        if t < 4:
            send(f"z{t}", "z", "C", ALL, y, k)
        else:
            send("x", "x", "C", X, y, k)
        yield
        take(f"x{k}", "B", x, ALL, k)
        if t > 1:
            take(f"z{t - 1}", "B", x, ALL, k)
        if t < 4:
            send(f"z{t}", "z", "B", x, ALL, k)
        else:
            send("y", "y", "B", x, Y, k)

    def third(k):
        t = k or 4
        take(f"x{k}", "A", x, y, k)
        if t > 1:
            take(f"z{t - 1}", "A", x, y, k)
        if t < 4:
            send(f"z{t}", "z", "A", x, y, k)

    for k, away in ((1, True), (2, True), (1, False), (3, True), (2, False), (0, True), (3, False), (0, False)):
        swap(k, away)
    yield
    far(1)
    yield
    far(2)
    yield
    swapped(1, False)
    yield
    yield from second(1)
    yield
    far(3)
    yield
    swapped(2, False)
    yield
    third(1)
    yield
    yield from second(2)
    yield
    far(0)
    yield
    swapped(3, False)
    yield
    third(2)
    yield
    yield from second(3)
    yield
    swapped(0, False)
    yield
    third(3)
    yield
    yield from second(0)
    yield
    third(0)
    yield
    take("x", "C", x, y, 0)
    yield
    take("y", "B", x, y, 0)


def scatter_scratch(M, N):
    return ([pltpu.VMEM((M, 2, 2, 4, 3, 8, FF), BF16), pltpu.VMEM((N, 2, 2, 4, 7, 8, D), BF16)] * 2
            + [pltpu.VMEM((M, ROOM, GU_UNITS[o][1], 8, FF), BF16) for o in "ABC"] + [pltpu.VMEM((N, ROOM, DN_UNITS[o][1], 8, D), BF16) for o in "ABC"])


def scatter_kernel(M, N, *refs):
    gus, dns = refs[:M], refs[M:M + N]
    gu_out, dn_out = refs[M + N:M + N + 2]
    gu, dn, sgu, sdn, ga, gb, gc, da, db, dc, send, recv, local = refs[M + N + 2:]
    x, y, z, c = place()
    greet()
    copies = Copies(send, recv)
    steps = scatter_steps(copies, gus, dns, gu, dn, sgu, sdn, {"A": (ga, da), "B": (gb, db), "C": (gc, dc)}, "")
    next(steps)
    loads = [pltpu.make_async_copy(gus[i].at[ALL, ALL, ALL, c], gu.at[i], local.at[i]) for i in range(M)]
    loads += [pltpu.make_async_copy(dns[i].at[ALL, ALL, ALL, c], dn.at[i], local.at[M + i]) for i in range(N)]
    for load in loads:
        load.start()
    for load in loads:
        load.wait()
    for _ in steps:
        pass
    stores = [pltpu.make_async_copy(gu.at[ALL, x, y, z], gu_out, local.at[0]), pltpu.make_async_copy(dn.at[ALL, x, y, z], dn_out, local.at[1])]
    for store in stores:
        store.start()
    for store in stores:
        store.wait()
    copies.finish()


def scatter(gus, dns, number=1):
    M, N = len(gus), len(dns)
    hbm = pl.BlockSpec(memory_space=pl.ANY)
    return pl.pallas_call(
        functools.partial(scatter_kernel, M, N), name="scatter",
        out_shape=(jax.ShapeDtypeStruct((M, 3, 8, FF), BF16), jax.ShapeDtypeStruct((N, 7, 8, D), BF16)),
        in_specs=[hbm] * (M + N), out_specs=(hbm, hbm),
        scratch_shapes=[*scatter_scratch(M, N), pltpu.SemaphoreType.DMA((SCATTER_COPIES,)), pltpu.SemaphoreType.DMA((SCATTER_COPIES,)), pltpu.SemaphoreType.DMA((M + N,))],
        compiler_params=pltpu.CompilerParams(collective_id=number, has_side_effects=True, vmem_limit_bytes=60 * 1024 * 1024),
    )(*gus, *dns)


def dot(a, b, ca, cb):
    return lax.dot_general(a, b, (((ca,), (cb,)), ((), ())), preferred_element_type=F32)


def compute(x, dy, wg, wu, wd):
    saved = []
    h = x
    for l in range(LAYERS):
        wide = h.astype(F32)
        s = lax.rsqrt(jnp.mean(wide**2, -1, keepdims=True) + 1e-6)
        a = (wide * s).astype(BF16)
        g, u = dot(a, wg[l], 1, 0), dot(a, wu[l], 1, 0)
        p = (jax.nn.silu(g) * u).astype(BF16)
        saved.append((h, s, a, g, u, p))
        if l < LAYERS - 1:
            h = h + dot(p, wd[l], 1, 0).astype(BF16)
    ct, grads = dy, [None] * LAYERS
    for l in reversed(range(LAYERS)):
        h, s, a, g, u, p = saved[l]
        by_down = dot(p, ct, 0, 0).astype(BF16)
        by_p = dot(ct, wd[l], 1, 1).astype(BF16).astype(F32)
        sig = jax.nn.sigmoid(g)
        by_u = (by_p * g * sig).astype(BF16)
        by_g = (by_p * u * (sig * (1 + g * (1 - sig)))).astype(BF16)
        by_gate, by_up = dot(a, by_g, 0, 0).astype(BF16), dot(a, by_u, 0, 0).astype(BF16)
        by_a = dot(by_g, wg[l], 1, 1) + dot(by_u, wu[l], 1, 1)
        n = h.astype(F32) * s
        ct = (ct.astype(F32) + s * (by_a - n * jnp.mean(by_a * n, -1, keepdims=True))).astype(BF16)
        grads[l] = (by_gate, by_up, by_down)
    return ct, grads


def solution(mesh):
    def step(x, dy, w_gate, w_up, w_down):
        gu_in = jnp.concatenate([w_gate, w_up]).reshape(4, 3, 8, FF)
        gu, dn = gather(gu_in, w_down.reshape(2, 7, 8, D))
        gu, dn = gu.reshape(4, D, FF), dn.reshape(2, FF, D)
        ct, grads = compute(x[0], dy[0], gu[:2], gu[2:], dn)
        gus = [grads[l][i].reshape(*GRID, 3, 8, FF) for i in (0, 1) for l in (0, 1)]
        dns = [grads[l][2].reshape(*GRID, 7, 8, D) for l in (0, 1)]
        by_gu, by_dn = scatter(gus, dns)
        by_gu = by_gu.reshape(4, 24, FF)
        return ct[None], by_gu[:2], by_gu[2:], by_dn.reshape(2, 56, D)

    rows = P(None, "dp", None)
    tokens = P(("rep", "dp"), None, None)
    return jax.shard_map(step, mesh=mesh, in_specs=(tokens, tokens, rows, rows, rows), out_specs=(tokens, P("rep", "dp", None), P("rep", "dp", None), P("rep", "dp", None)), check_vma=False)
```

time: 1660 us -> 403 us (0.24)
  starting transfers between devices: 554 us -> 0 us
  matrix products: 495 us -> 189 us
  other arithmetic: 294 us -> 11 us
  waiting for transfers between devices: 183 us -> 0 us
  Pallas kernels: 0 us -> 172 us
  local copies, waits for them, and re-layouts: 95.3 us -> 21.9 us
    dot_general x231 -> x0, starting transfers between devices: 554 us -> none  [the longest x99 212 us: matmul(): jnp.dot(a, w, preferred_element_type=jnp.float32).astype(jnp.bfloat16)]
    dot_general x122 -> x17, matrix products: 495 us -> 189 us  [dot(): lax.dot_general(a, b, (((ca,), (cb,)), ((), ())), preferred_element_type=...]
    dot_general x192 -> x0, other arithmetic: 260 us -> none
    pallas_call x0 -> x2, Pallas kernels: none -> 172 us  [the longest x1 96.7 us: scatter(): pl.pallas_call(functools.partial(scatter_kernel, M, N), name='scatter', o...]
    dot_general x231 -> x0, waiting for transfers between devices: 157 us -> none  [the longest x99 150 us: matmul(): jnp.dot(a, w, preferred_element_type=jnp.float32).astype(jnp.bfloat16)]
    dot_general x66 -> x0, local copies, waits for them, and re-layouts: 51.8 us -> none  [the longest x34 51.8 us: matmul(): jnp.dot(a, w, preferred_element_type=jnp.float32).astype(jnp.bfloat16)]
    unnamed x56 -> x60, local copies, waits for them, and re-layouts: 38.6 us -> 11.9 us
    squeeze x5 -> x0, waiting for transfers between devices: 25.8 us -> none  [stack(): h = layer(h, {name: w[number] for name, w in weights.items()})]
  transfers between devices with their start and end apart: 236 -> 0, of which waited for: 74 -> 0; matrix products, arithmetic and copies ran while one was open for 51% -> 0% of each run, Pallas kernels for 0% -> 0%
where the time goes in v1:
time: 403 us; the launch traced here: 396 us
  matrix products  189 us (47%)
  Pallas kernels  172 us (43%)
  local copies, waits for them, and re-layouts  21.9 us (5%)
  other arithmetic  11 us (3%)
    dot_general x17, matrix products, dot(): lax.dot_general(a, b, (((ca,), (cb,)), ((), ())), preferred_element_type=...  189 us
    pallas_call x1, Pallas kernels, scatter(): pl.pallas_call(functools.partial(scatter_kernel, M, N), name='scatter', o...  96.7 us
    pallas_call x1, Pallas kernels, gather(): pl.pallas_call(gather_kernel, name='gather', out_shape=(jax.ShapeDtypeStr...  75.4 us
    unnamed x60, local copies, waits for them, and re-layouts  11.9 us

profile of v1, /device:TPU:0, one launch (start us, length us, event | category | flops | bytes accessed | tf_op | source)
XLA Modules:
  0.0 395.7 jit_solution(14832823847143739975)
XLA Ops:
  0.6 0.0 copy-start.16
  0.6 0.0 copy-start.15
  0.7 3.2 copy.10
  3.9 0.0 copy-start
  3.9 0.7 fusion.20
  4.6 0.0 copy-done.16
  4.6 0.0 copy-done.15
  4.6 0.0 copy-start.18
  4.6 1.1 maximum_bitcast_fusion.gu_in
  5.7 75.4 %gather.1 = (bf16[4,2,2,4,2,3,8,1792]{7,6,5,4,3,2,1,0:T(8,128)(2,1)}, bf16[2,2,2,4,2,7,8,768]{7,6,5,4,3,2,1,0:T(8,128)(2,1)}) custom-call(bf16[4,3,8,1792]{3,2,1,0:T(8,128)(2,1)} %maximum_bitcast_fusion.gu_in, bf16[2,7,8,768]{3,2,1,0:T(8,128)(2,1)} %bitcast.97), custom_call_target="tpu_custom_call" | custom-call | tf_op jit(solution)/shard_map/gather/pallas_call | solution.py:195
  81.1 0.0 copy-start.4
  81.1 7.7 %fusion.45 = (bf16[1,2,2,4,2,3,8,1792]{7,6,5,4,3,2,1,0:T(8,128)(2,1)}, bf16[1,2,2,4,2,3,8,1792]{7,6,5,4,3,2,1,0:T(8,128)(2,1)}, bf16[1,2,2,4,2,3,8,1792]{7,6,5,4...) fusion(bf16[4,2,2,4,2,3,8,1792]{7,6,5,4,3,2,1,0:T(8,128)(2,1)} %get-tuple-element.8), kind=kLoop, calls=%fused_computation.68 | loop fusion | bytes 22020096 | tf_op jit(solution)/shard_map/slice | solution.py:397
  88.8 0.0 copy-done.4
  88.8 0.0 slice-start
  88.9 9.2 %fusion.42 = f32[2048,1792]{1,0:T(8,128)} fusion(bf16[768,1792]{1,0:T(8,128)(2,1)S(1)} %bitcast.85, bf16[1,2048,768]{2,1,0:T(8,128)(2,1)S(1)} %copy-done.4, f32[2048]{0:T(1024)S(1)} %add_rsqrt_fusion.1), kind=kOutput, calls=%fused_computation.59 | convolution fusion | flops 5641863168 | bytes 20586496 | tf_op jit(solution)/shard_map/dot_general | solution.py:387
  98.1 0.0 copy-done.11
  98.1 0.0 copy-done.18
  98.1 15.3 %multiply_convert_fusion.1 = (bf16[2048,1792]{1,0:T(8,128)(2,1)}, f32[2048,1792]{1,0:T(8,128)}) fusion(f32[2048,1792]{1,0:T(8,128)} %fusion.42, bf16[768,1792]{1,0:T(8,128)(2,1)} %bitcast.83, bf16[1,2048,768]{2,1,0:T(8,128)(2,1)} %param.5, f32[2048]{0:T(1024)S(1)} %add_rsqrt_fusion.1), kind=kOutput, calls=%fused_computation.14 | convolution fusion | flops 5663883264 | bytes 42606592 | tf_op jit(solution)/shard_map/dot_general | solution.py:387
  113.3 0.0 slice-done
  113.3 0.0 slice-done.1
  113.3 0.5 fusion.46
  113.9 0.0 copy-start.9
  113.9 0.0 copy-done
  113.9 0.0 copy-start.12
  113.9 10.0 %fusion.26 = (f32[2048]{0:T(1024)S(1)}, bf16[2048,768]{0,1:T(8,128)(2,1)S(1)}) fusion(bf16[2048,1792]{1,0:T(8,128)(2,1)} %get-tuple-element.28, bf16[1792,768]{1,0:T(8,128)(2,1)S(1)} %bitcast.80, bf16[1,2048,768]{1,2,0:T(8,128)(2,1)S(1)} %copy.10), kind=kOutput, calls=%fused_computation.40 | convolution fusion | flops 5645006848 | bytes 16392192 | tf_op jit(solution)/shard_map/dot_general | solution.py:387
  123.9 0.0 copy-done.9
  123.9 0.0 copy-start.6
  123.9 0.0 copy-done.12
  123.9 0.0 copy-start.5
  123.9 9.2 %fusion.38 = f32[2048,1792]{1,0:T(8,128)} fusion(bf16[768,1792]{1,0:T(8,128)(2,1)S(1)} %bitcast.88, bf16[2048,768]{0,1:T(8,128)(2,1)S(1)} %get-tuple-element.31, f32[2048]{0:T(1024)S(1)} %add_rsqrt_fusion), kind=kOutput, calls=%fused_computation.57 | convolution fusion | flops 5641863168 | bytes 20586496 | tf_op jit(solution)/shard_map/dot_general | solution.py:387
  133.1 0.0 copy-done.5
  133.1 8.1 %convolution_convert_fusion.1 = bf16[1792,2048]{0,1:T(8,128)(2,1)} fusion(bf16[1792,768]{1,0:T(8,128)(2,1)S(1)} %bitcast.82, bf16[1,2048,768]{2,1,0:T(8,128)(2,1)S(1)} %copy-done.5), kind=kOutput, calls=%fused_computation.27 | convolution fusion | flops 5640814592 | bytes 13238272 | tf_op jit(solution)/shard_map/dot_general | solution.py:387
  141.3 23.3 %fusion.7 = (bf16[2048,1792]{1,0:T(8,128)(2,1)}, bf16[2048,1792]{1,0:T(8,128)(2,1)}, f32[2048,1792]{1,0:T(8,128)}) fusion(bf16[1792,2048]{0,1:T(8,128)(2,1)} %convolution_convert_fusion.1, f32[2048,1792]{1,0:T(8,128)} %fusion.38, bf16[768,1792]{1,0:T(8,128)(2,1)} %bitcast.90, bf16[2048,768]{0,1:T(8,128)(2,1)} %copy-done.6, f32[2048]{0:T(1024)S(1)} %add_rsqrt_fusion), kind=kOutput, calls=%fused_computation.11 | convolution fusion | flops 5693243392 | bytes 57286656 | tf_op jit(solution)/shard_map/dot_general | solution.py:387
  164.6 14.1 %fusion.27 = bf16[1792,768]{1,0:T(8,128)(2,1)} fusion(f32[2048,1792]{1,0:T(8,128)} %fusion.38, f32[2048,1792]{1,0:T(8,128)} %get-tuple-element.32, bf16[1,2048,768]{2,1,0:T(8,128)(2,1)S(1)} %copy-done.5), kind=kOutput, calls=%fused_computation.50 | convolution fusion | flops 5660540928 | bytes 35258368 | tf_op jit(solution)/shard_map/dot_general | solution.py:387
  178.7 8.3 %fusion.47 = f32[2048,768]{0,1:T(8,128)S(1)} fusion(bf16[2048,1792]{1,0:T(8,128)(2,1)} %get-tuple-element.19, bf16[768,1792]{1,0:T(8,128)(2,1)S(1)} %bitcast.91), kind=kOutput, calls=%fused_computation.70 | convolution fusion | flops 5637144576 | bytes 16384000 | tf_op jit(solution)/shard_map/dot_general | solution.py:387
  187.0 0.0 copy-done.7
  187.0 0.0 copy-done.13
  187.1 0.0 copy-done.21
  187.1 8.1 %fusion.21 = (f32[2048]{0:T(1024)S(1)}, f32[2048,768]{0,1:T(8,128)}) fusion(bf16[2048,768]{0,1:T(8,128)(2,1)S(1)} %copy-done.7, f32[2048]{0:T(1024)S(1)} %add_rsqrt_fusion, f32[2048,768]{0,1:T(8,128)S(1)} %fusion.47, bf16[2048,1792]{1,0:T(8,128)(2,1)S(1)} %copy-done.21, bf16[768,1792]{1,0:T(8,128)(2,1)S(1)} %bitcast.89), kind=kOutput, calls=%fused_computation.35 | convolution fusion | flops 5645006848 | bytes 25837568 | tf_op jit(solution)/shard_map/dot_general | solution.py:387
  195.2 3.2 copy.9
  198.4 0.0 slice-start.2
  198.4 0.0 slice-start.4
  198.4 5.7 %fusion.25 = bf16[2048,768]{0,1:T(8,128)(2,1)S(1)} fusion(f32[2048,768]{0,1:T(8,128)} %get-tuple-element.34, bf16[2048,768]{0,1:T(8,128)(2,1)} %copy-done.6, bf16[1,2048,768]{1,2,0:T(8,128)(2,1)S(1)} %copy.9, f32[2048]{0:T(1024)S(1)} %broadcast_multiply_fusion.1, f32[2048]{0:T(1024)S(1)} %add_rsqrt_fusion), kind=kLoop, calls=%fused_computation.39 | loop fusion | flops 12582912 | bytes 15745024 | tf_op jit(solution)/shard_map/convert_element_type | solution.py:413
  204.1 0.0 slice-start.3
  204.1 0.0 slice-start.5
  204.1 10.5 %convolution_convert_fusion.2 = bf16[1792,768]{1,0:T(8,128)(2,1)} fusion(bf16[2048,1792]{1,0:T(8,128)(2,1)} %get-tuple-element.28, bf16[2048,768]{0,1:T(8,128)(2,1)S(1)} %fusion.25), kind=kOutput, calls=%fused_computation.44 | convolution fusion | flops 5638520832 | bytes 13238272 | tf_op jit(solution)/shard_map/dot_general | solution.py:387
  214.6 0.0 copy-done.2
  214.7 7.3 %convolution_convert_fusion.3 = bf16[768,1792]{1,0:T(8,128)(2,1)} fusion(bf16[2048,1792]{1,0:T(8,128)(2,1)S(1)} %bitcast.100, bf16[2048,768]{0,1:T(8,128)(2,1)S(1)} %copy-done.8, f32[2048]{0:T(1024)S(1)} %add_rsqrt_fusion), kind=kOutput, calls=%fused_computation.45 | convolution fusion | flops 5643239424 | bytes 13246464 | tf_op jit(solution)/shard_map/dot_general | solution.py:387
  222.0 0.0 slice-done.5
  222.0 7.2 %convolution_convert_fusion.5 = bf16[768,1792]{1,0:T(8,128)(2,1)} fusion(bf16[2048,1792]{1,0:T(8,128)(2,1)S(1)} %bitcast.102, bf16[2048,768]{0,1:T(8,128)(2,1)S(1)} %copy-done.8, f32[2048]{0:T(1024)S(1)} %add_rsqrt_fusion), kind=kOutput, calls=%fused_computation.47 | convolution fusion | flops 5643239424 | bytes 13246464 | tf_op jit(solution)/shard_map/dot_general | solution.py:387
  229.2 23.3 %fusion.3 = (bf16[2048,1792]{1,0:T(8,128)(2,1)}, bf16[2048,1792]{1,0:T(8,128)(2,1)}) fusion(f32[2048,1792]{1,0:T(8,128)} %fusion.42, f32[2048,1792]{1,0:T(8,128)} %get-tuple-element.29, bf16[2048,768]{0,1:T(8,128)(2,1)} %copy-done.2, bf16[1792,768]{1,0:T(8,128)(2,1)} %bitcast.81), kind=kOutput, calls=%fused_computation.5 | convolution fusion | flops 5692194816 | bytes 49938432 | tf_op jit(solution)/shard_map/dot_general | solution.py:387
  252.5 0.0 copy-start.20
  252.5 10.4 %convolution_convert_fusion.6 = bf16[768,1792]{1,0:T(8,128)(2,1)} fusion(bf16[2048,1792]{1,0:T(8,128)(2,1)} %get-tuple-element.17, bf16[1,2048,768]{1,2,0:T(8,128)(2,1)S(1)} %copy-done.1, f32[2048]{0:T(1024)S(1)} %copy-done.19), kind=kOutput, calls=%fused_computation.48 | convolution fusion | flops 5643239424 | bytes 13246464 | tf_op jit(solution)/shard_map/dot_general | solution.py:387
  262.9 7.2 %convolution_convert_fusion.4 = bf16[768,1792]{1,0:T(8,128)(2,1)} fusion(bf16[2048,1792]{1,0:T(8,128)(2,1)S(1)} %copy-done.20, bf16[1,2048,768]{1,2,0:T(8,128)(2,1)S(1)} %copy-done.1, f32[2048]{0:T(1024)S(1)} %copy-done.19), kind=kOutput, calls=%fused_computation.46 | convolution fusion | flops 5643239424 | bytes 13246464 | tf_op jit(solution)/shard_map/dot_general | solution.py:387
  270.1 96.7 %scatter.1 = (bf16[4,3,8,1792]{3,2,1,0:T(8,128)(2,1)}, bf16[2,7,8,768]{3,2,1,0:T(8,128)(2,1)}) custom-call(bf16[2,2,4,2,3,8,1792]{6,5,4,3,2,1,0:T(8,128)(2,1)} %bitcast.95, bf16[2,2,4,2,3,8,1792]{6,5,4,3,2,1,0:T(8,128)(2,1)} %bitcast.94, bf16[2,2,4,2,3,8,1792]{6,5,4,3,2,1,0:T(8,128)(2,1)} %bitcast.96, bf16[2,2,4,2,3,8,1792]{6,5,4,3,2,1,0:T(8,128)(2,1)} %bitcast.93, ...), custom_call_target="tpu_custom_call" | custom-call | tf_op jit(solution)/shard_map/scatter/pallas_call | solution.py:377
  366.8 1.8 slice_bitcast_fusion
  368.6 9.1 %fusion.48 = f32[2048,768]{0,1:T(8,128)S(1)} fusion(bf16[2048,1792]{1,0:T(8,128)(2,1)} %get-tuple-element.17, bf16[768,1792]{1,0:T(8,128)(2,1)} %bitcast.86), kind=kOutput, calls=%fused_computation.71 | convolution fusion | flops 5637144576 | bytes 16384000 | tf_op jit(solution)/shard_map/dot_general | solution.py:387
  377.7 0.0 copy-done.10
  377.7 0.0 copy-start.3
  377.7 8.6 %fusion.15 = (f32[2048]{0:T(1024)S(1)}, f32[2048,768]{0,1:T(8,128)S(1)}) fusion(bf16[1,2048,768]{1,2,0:T(8,128)(2,1)S(1)} %copy-done.1, f32[2048]{0:T(1024)S(1)} %copy-done.19, f32[2048,768]{0,1:T(8,128)S(1)} %fusion.48, bf16[2048,1792]{1,0:T(8,128)(2,1)} %get-tuple-element.16, bf16[768,1792]{1,0:T(8,128)(2,1)S(1)} %bitcast.84), kind=kOutput, calls=%fused_computation.29 | convolution fusion | flops 5645006848 | bytes 25837568 | tf_op jit(solution)/shard_map/dot_general | solution.py:387
  386.3 0.0 copy-done.3
  386.3 3.5 fusion.29
  389.9 4.7 %copy.12 = bf16[1,2048,768]{2,1,0:T(8,128)(2,1)} copy(bf16[1,2048,768]{1,2,0:T(8,128)(2,1)} %fusion.29) | data formatting | bytes 6291456
  394.6 0.7 copy.15
  (29 shorter events, 0.1 us)
Async XLA Ops:
  0.6 4.0 copy-start.16
  0.6 4.0 copy-start.15
  3.9 110.0 %copy-start = (bf16[1,2048,768]{1,2,0:T(8,128)(2,1)}, bf16[1,2048,768]{1,2,0:T(8,128)(2,1)S(1)}, u32[]{:S(2)}) copy-start(bf16[1,2048,768]{1,2,0:T(8,128)(2,1)S(1)} %copy.10) | copy-start | bytes 9437188
  4.6 93.5 %copy-start.18 = (f32[2048]{0:T(1024)}, f32[2048]{0:T(1024)S(1)}, u32[]{:S(2)}) copy-start(f32[2048]{0:T(1024)S(1)} %add_rsqrt_fusion.1) | copy-start | bytes 24580
  81.1 7.7 %copy-start.4 = (bf16[1,2048,768]{2,1,0:T(8,128)(2,1)S(1)}, bf16[1,2048,768]{2,1,0:T(8,128)(2,1)}, u32[]{:S(2)}) copy-start(bf16[1,2048,768]{2,1,0:T(8,128)(2,1)} %param.5) | copy-start | bytes 9437188
  88.8 9.2 %copy-start.11 = (bf16[1,2,2,4,2,3,8,1792]{7,6,5,4,3,2,1,0:T(8,128)(2,1)}, bf16[1,2,2,4,2,3,8,1792]{7,6,5,4,3,2,1,0:T(8,128)(2,1)S(1)}, u32[]{:S(2)}) copy-start(bf16[1,2,2,4,2,3,8,1792]{7,6,5,4,3,2,1,0:T(8,128)(2,1)S(1)} %get-tuple-element.23) | copy-start | bytes 8257540
  88.8 24.5 %slice-start = ((s8[5505024]{0:T(1024)(128)(4,1)}), s8[4194304]{0:T(1024)(128)(4,1)S(1)}, s32[]{:S(2)}) async-start(s8[5505024]{0:T(1024)(128)(4,1)} %bitcast.78), calls=%async_computation | async-start | bytes 8388608
  98.1 15.3 %slice-start.1 = ((s8[5505024]{0:T(1024)(128)(4,1)}), s8[1310720]{0:T(1024)(128)(4,1)S(1)}, s32[]{:S(2)}) async-start(s8[5505024]{0:T(1024)(128)(4,1)} %bitcast.78), calls=%async_computation.1 | async-start | bytes 2621440
  113.9 10.0 %copy-start.9 = (bf16[1,2,2,4,2,7,8,768]{7,6,5,4,3,2,1,0:T(8,128)(2,1)}, bf16[1,2,2,4,2,7,8,768]{7,6,5,4,3,2,1,0:T(8,128)(2,1)S(1)}, u32[]{:S(2)}) copy-start(bf16[1,2,2,4,2,7,8,768]{7,6,5,4,3,2,1,0:T(8,128)(2,1)S(1)} %get-tuple-element.25) | copy-start | bytes 8257540
  113.9 10.0 %copy-start.12 = (bf16[1,2,2,4,2,3,8,1792]{7,6,5,4,3,2,1,0:T(8,128)(2,1)S(1)}, bf16[1,2,2,4,2,3,8,1792]{7,6,5,4,3,2,1,0:T(8,128)(2,1)}, u32[]{:S(2)}) copy-start(bf16[1,2,2,4,2,3,8,1792]{7,6,5,4,3,2,1,0:T(8,128)(2,1)} %get-tuple-element.21) | copy-start | bytes 8257540
  123.9 9.2 %copy-start.6 = (bf16[2048,768]{0,1:T(8,128)(2,1)}, bf16[2048,768]{0,1:T(8,128)(2,1)S(1)}, u32[]{:S(2)}) copy-start(bf16[2048,768]{0,1:T(8,128)(2,1)S(1)} %get-tuple-element.31) | copy-start | bytes 9437188
  123.9 9.2 %copy-start.5 = (bf16[1,2048,768]{2,1,0:T(8,128)(2,1)S(1)}, bf16[1,2048,768]{2,1,0:T(8,128)(2,1)}, u32[]{:S(2)}) copy-start(bf16[1,2048,768]{2,1,0:T(8,128)(2,1)} %param.6) | copy-start | bytes 9437188
  164.6 14.1 %copy-start.14 = (bf16[1,2,2,4,2,3,8,1792]{7,6,5,4,3,2,1,0:T(8,128)(2,1)S(1)}, bf16[1,2,2,4,2,3,8,1792]{7,6,5,4,3,2,1,0:T(8,128)(2,1)}, u32[]{:S(2)}) copy-start(bf16[1,2,2,4,2,3,8,1792]{7,6,5,4,3,2,1,0:T(8,128)(2,1)} %get-tuple-element.20) | copy-start | bytes 8257540
  178.7 8.3 %copy-start.7 = (bf16[2048,768]{0,1:T(8,128)(2,1)S(1)}, bf16[2048,768]{0,1:T(8,128)(2,1)}, u32[]{:S(2)}) copy-start(bf16[2048,768]{0,1:T(8,128)(2,1)} %copy-done.6) | copy-start | bytes 9437188
  178.7 8.3 %copy-start.13 = (bf16[1,2,2,4,2,3,8,1792]{7,6,5,4,3,2,1,0:T(8,128)(2,1)S(1)}, bf16[1,2,2,4,2,3,8,1792]{7,6,5,4,3,2,1,0:T(8,128)(2,1)}, u32[]{:S(2)}) copy-start(bf16[1,2,2,4,2,3,8,1792]{7,6,5,4,3,2,1,0:T(8,128)(2,1)} %get-tuple-element.21) | copy-start | bytes 8257540
  178.7 8.3 %copy-start.21 = (bf16[2048,1792]{1,0:T(8,128)(2,1)S(1)}, bf16[2048,1792]{1,0:T(8,128)(2,1)}, u32[]{:S(2)}) copy-start(bf16[2048,1792]{1,0:T(8,128)(2,1)} %get-tuple-element.18) | copy-start | bytes 22020100
  198.4 16.3 %slice-start.2 = ((s8[7340032]{0:T(1024)(128)(4,1)}), s8[4194304]{0:T(1024)(128)(4,1)S(1)}, s32[]{:S(2)}) async-start(s8[7340032]{0:T(1024)(128)(4,1)} %bitcast.99), calls=%async_computation.2 | async-start | bytes 8388608
  198.4 23.6 %slice-start.4 = ((s8[7340032]{0:T(1024)(128)(4,1)}), s8[4194304]{0:T(1024)(128)(4,1)S(1)}, s32[]{:S(2)}) async-start(s8[7340032]{0:T(1024)(128)(4,1)} %bitcast.101), calls=%async_computation.4 | async-start | bytes 8388608
  204.1 10.5 %copy-start.2 = (bf16[2048,768]{0,1:T(8,128)(2,1)}, bf16[2048,768]{0,1:T(8,128)(2,1)S(1)}, u32[]{:S(2)}) copy-start(bf16[2048,768]{0,1:T(8,128)(2,1)S(1)} %fusion.25) | copy-start | bytes 9437188
  204.1 10.5 %copy-start.8 = (bf16[2048,768]{0,1:T(8,128)(2,1)S(1)}, bf16[2048,768]{0,1:T(8,128)(2,1)}, u32[]{:S(2)}) copy-start(bf16[2048,768]{0,1:T(8,128)(2,1)} %copy-done.6) | copy-start | bytes 9437188
  204.1 10.5 %slice-start.3 = ((s8[7340032]{0:T(1024)(128)(4,1)}), s8[3145728]{0:T(1024)(128)(4,1)S(1)}, s32[]{:S(2)}) async-start(s8[7340032]{0:T(1024)(128)(4,1)} %bitcast.99), calls=%async_computation.3 | async-start | bytes 6291456
  204.1 17.8 %slice-start.5 = ((s8[7340032]{0:T(1024)(128)(4,1)}), s8[3145728]{0:T(1024)(128)(4,1)S(1)}, s32[]{:S(2)}) async-start(s8[7340032]{0:T(1024)(128)(4,1)} %bitcast.101), calls=%async_computation.5 | async-start | bytes 6291456
  229.2 23.3 %copy-start.1 = (bf16[1,2048,768]{1,2,0:T(8,128)(2,1)S(1)}, bf16[1,2048,768]{1,2,0:T(8,128)(2,1)}, u32[]{:S(2)}) copy-start(bf16[1,2048,768]{1,2,0:T(8,128)(2,1)} %copy-done) | copy-start | bytes 9437188
  229.2 23.3 %copy-start.19 = (f32[2048]{0:T(1024)S(1)}, f32[2048]{0:T(1024)}, u32[]{:S(2)}) copy-start(f32[2048]{0:T(1024)} %copy-done.18) | copy-start | bytes 24580
  252.5 10.4 %copy-start.20 = (bf16[2048,1792]{1,0:T(8,128)(2,1)S(1)}, bf16[2048,1792]{1,0:T(8,128)(2,1)}, u32[]{:S(2)}) copy-start(bf16[2048,1792]{1,0:T(8,128)(2,1)} %get-tuple-element.16) | copy-start | bytes 22020100
  368.6 9.1 %copy-start.10 = (bf16[1,2,2,4,2,3,8,1792]{7,6,5,4,3,2,1,0:T(8,128)(2,1)S(1)}, bf16[1,2,2,4,2,3,8,1792]{7,6,5,4,3,2,1,0:T(8,128)(2,1)}, u32[]{:S(2)}) copy-start(bf16[1,2,2,4,2,3,8,1792]{7,6,5,4,3,2,1,0:T(8,128)(2,1)} %get-tuple-element.22) | copy-start | bytes 8257540
  377.7 8.6 %copy-start.3 = (bf16[2048,768]{0,1:T(8,128)(2,1)S(1)}, bf16[2048,768]{0,1:T(8,128)(2,1)}, u32[]{:S(2)}) copy-start(bf16[2048,768]{0,1:T(8,128)(2,1)} %copy-done.2) | copy-start | bytes 9437188
  389.9 4.7 %copy-start.17 = (bf16[2,7,8,768]{3,2,1,0:T(8,128)(2,1)S(1)}, bf16[2,7,8,768]{3,2,1,0:T(8,128)(2,1)}, u32[]{:S(2)}) copy-start(bf16[2,7,8,768]{3,2,1,0:T(8,128)(2,1)} %get-tuple-element.11) | copy-start | bytes 516100

commit v2 on v1

--- a/solution.py
+++ b/solution.py
@@ -48,24 +48,25 @@
     def __init__(self, send, recv):
         self.send, self.recv, self.made, self.used = send, recv, {}, 0
 
+    def group(self, name):
+        first, pairs, to = self.made[name]
+        return [pltpu.make_async_remote_copy(src_ref=src, dst_ref=dst, send_sem=self.send.at[first + i], recv_sem=self.recv.at[first + i],
+                                             device_id={"dp": to}, device_id_type=pl.DeviceIdType.MESH) for i, (src, dst) in enumerate(pairs())]
+
     def start(self, name, pairs, to):
-        made = []
-        for src, dst in pairs:
-            copy = pltpu.make_async_remote_copy(src_ref=src, dst_ref=dst, send_sem=self.send.at[self.used], recv_sem=self.recv.at[self.used],
-                                                device_id={"dp": to}, device_id_type=pl.DeviceIdType.MESH)
+        assert name not in self.made
+        self.made[name] = (self.used, pairs, to)
+        for copy in self.group(name):
             copy.start()
-            made.append(copy)
             self.used += 1
-        assert name not in self.made
-        self.made[name] = made
 
     def wait(self, name):
-        for copy in self.made[name]:
+        for copy in self.group(name):
             copy.wait_recv()
 
     def finish(self):
-        for made in self.made.values():
-            for copy in made:
+        for name in self.made:
+            for copy in self.group(name):
                 copy.wait_send()
 
 
@@ -91,16 +92,19 @@
         return (gu_in.at[gs, pl.ds(a, n)], dn_in.at[ds, pl.ds(b, m)])
 
     def send(name, way, colour, xs, ys, k, mine=False):
-        dst = region(colour, xs, ys, k)
-        src = own(colour) if mine else dst
-        copies.start(tag + colour + name, tuple(zip(src, dst)), to[way])
+        def pairs():
+            dst = region(colour, xs, ys, k)
+            return list(zip(own(colour) if mine else dst, dst))
+        copies.start(tag + colour + name, pairs, to[way])
 
     def arrived(name, colour, xs, ys, k):
         copies.wait(tag + colour + name)
 
     def share(name, colour, xs, ys, k):
-        reg = region(colour, xs, ys, k)
-        copies.start(tag + colour + name + "s", tuple(zip(reg, reg)), to["c"])
+        def pairs():
+            reg = region(colour, xs, ys, k)
+            return list(zip(reg, reg))
+        copies.start(tag + colour + name + "s", pairs, to["c"])
         shared.append((tag + colour + name + "s"))
 
     shared = []
@@ -109,8 +113,7 @@
     send("z1", "z", "A", x, y, 0, True)
     send("x0", "x", "A", x, y, 0, True)
     send("y0", "y", "A", x, y, 0, True)
-    full = (gu.at[gs, x, y, z, c], dn.at[ds, x, y, z, c])
-    copies.start(tag + "own", tuple(zip((gu_in.at[gs], dn_in.at[ds]), full)), to["c"])
+    copies.start(tag + "own", lambda: [(gu_in.at[gs], gu.at[gs, x, y, z, c]), (dn_in.at[ds], dn.at[ds, x, y, z, c])], to["c"])
     shared.append(tag + "own")
     yield
     yield
@@ -202,7 +205,7 @@
     )(gu_in, dn_in)
 
 
-SCATTER_COPIES = 700
+SCATTER_COPIES = 300
 ROOM = 15
 
 
@@ -214,14 +217,14 @@
     lax.fori_loop(0, count, body, 0)
 
 
-def scatter_steps(copies, gus, dns, gu, dn, sgu, sdn, arrive, tag):
+def scatter_steps(copies, M, N, gus, dns, gu, dn, sgu, sdn, arrive, tag):
     x, y, z, c = place()
     X, Y = 1 - x, 1 - y
     ring = [z]
     for _ in range(3):
         ring.append(before(ring[-1]))
     to = {"x": index(X, y, z, c), "y": index(x, Y, z, c), "z": index(x, y, after(z), c), "c": index(x, y, z, 1 - c)}
-    M, N = len(gus), len(dns)
+    other = 1 - c
     slots, used = {}, {"A": 0, "B": 0, "C": 0}
 
     def half(colour, far):
@@ -236,8 +239,10 @@
         for colour in "ACB":
             xs, ys = half(colour, far)
             (a, n), (b, m) = GU_UNITS[colour], DN_UNITS[colour]
-            pairs = [(gus[i].at[xs, ys, ring[k], 1 - c, pl.ds(a, n)], sgu.at[i, xs, ys, ring[k], pl.ds(a, n)]) for i in range(M)]
-            pairs += [(dns[i].at[xs, ys, ring[k], 1 - c, pl.ds(b, m)], sdn.at[i, xs, ys, ring[k], pl.ds(b, m)]) for i in range(N)]
+
+            def pairs(xs=xs, ys=ys, a=a, n=n, b=b, m=m):
+                return ([(gus(i).at[xs, ys, ring[k], other, pl.ds(a, n)], sgu.at[i, xs, ys, ring[k], pl.ds(a, n)]) for i in range(M)]
+                        + [(dns(i).at[xs, ys, ring[k], other, pl.ds(b, m)], sdn.at[i, xs, ys, ring[k], pl.ds(b, m)]) for i in range(N)])
             copies.start(f"{tag}s{colour}{k}{far}", pairs, to["c"])
 
     def swapped(k, far):
@@ -254,10 +259,12 @@
         at = used[colour]
         used[colour] += number
         slots[colour + name] = at
-        to_at = pl.ds(at, number) if number == 2 else at
         rgu, rdn = arrive[colour]
-        copies.start(tag + colour + name, [(gu.at[ALL, xs, ys, ring[k], pl.ds(a, n)], rgu.at[ALL, to_at]),
-                                           (dn.at[ALL, xs, ys, ring[k], pl.ds(b, m)], rdn.at[ALL, to_at])], to[way])
+
+        def pairs():
+            to_at = pl.ds(at, number) if number == 2 else at
+            return [(gu.at[ALL, xs, ys, ring[k], pl.ds(a, n)], rgu.at[ALL, to_at]), (dn.at[ALL, xs, ys, ring[k], pl.ds(b, m)], rdn.at[ALL, to_at])]
+        copies.start(tag + colour + name, pairs, to[way])
 
     def take(name, colour, xs, ys, k):
         copies.wait(tag + colour + name)
@@ -301,6 +308,7 @@
         if t < 4:
             send(f"z{t}", "z", "A", x, y, k)
 
+    yield
     for k, away in ((1, True), (2, True), (1, False), (3, True), (2, False), (0, True), (3, False), (0, False)):
         swap(k, away)
     yield
@@ -346,73 +354,212 @@
             + [pltpu.VMEM((M, ROOM, GU_UNITS[o][1], 8, FF), BF16) for o in "ABC"] + [pltpu.VMEM((N, ROOM, DN_UNITS[o][1], 8, D), BF16) for o in "ABC"])
 
 
-def scatter_kernel(M, N, *refs):
-    gus, dns = refs[:M], refs[M:M + N]
-    gu_out, dn_out = refs[M + N:M + N + 2]
-    gu, dn, sgu, sdn, ga, gb, gc, da, db, dc, send, recv, local = refs[M + N + 2:]
+TILE, CHUNK = 256, 512
+TILES, CHUNKS = FF // TILE, TOKENS // CHUNK
+MIB = 1024 * 1024
+
+
+def dot(a, b, ca, cb):
+    return lax.dot_general(a, b, (((ca,), (cb,)), ((), ())), preferred_element_type=F32)
+
+
+def back_kernel(dy, h0, h1, wgu, wd, g0, u0, g1, u1, dx, gu_out, dn_out, gus, dns, *scratch):
+    (ct, hbuf, at, acc, gate, up, wgu_t, wd_t, p, dgu, stage, stage_dn,
+     gu1, dn1, sgu1, sdn1, ga1, gb1, gc1, da1, db1, dc1, gu0_, dn0_, sgu0, sdn0, ga0, gb0, gc0, da0, db0, dc0,
+     send1, recv1, send0, recv0, sem_in, sem_h, sem_out, sem_own) = scratch
     x, y, z, c = place()
     greet()
-    copies = Copies(send, recv)
-    steps = scatter_steps(copies, gus, dns, gu, dn, sgu, sdn, {"A": (ga, da), "B": (gb, db), "C": (gc, dc)}, "")
-    next(steps)
-    loads = [pltpu.make_async_copy(gus[i].at[ALL, ALL, ALL, c], gu.at[i], local.at[i]) for i in range(M)]
-    loads += [pltpu.make_async_copy(dns[i].at[ALL, ALL, ALL, c], dn.at[i], local.at[M + i]) for i in range(N)]
-    for load in loads:
-        load.start()
-    for load in loads:
-        load.wait()
-    for _ in steps:
-        pass
-    stores = [pltpu.make_async_copy(gu.at[ALL, x, y, z], gu_out, local.at[0]), pltpu.make_async_copy(dn.at[ALL, x, y, z], dn_out, local.at[1])]
-    for store in stores:
-        store.start()
-    for store in stores:
-        store.wait()
-    copies.finish()
-
-
-def scatter(gus, dns, number=1):
-    M, N = len(gus), len(dns)
+
+    def terms(l, i):
+        return gus.at[2 * i + l].reshape(*GRID, 3, 8, FF)
+
+    def terms_dn(l, i):
+        return dns.at[l].reshape(*GRID, 7, 8, D)
+
+    runs = {}
+    for l, (gu, dn, sgu, sdn, arrive, send, recv) in {
+        1: (gu1, dn1, sgu1, sdn1, {"A": (ga1, da1), "B": (gb1, db1), "C": (gc1, dc1)}, send1, recv1),
+        0: (gu0_, dn0_, sgu0, sdn0, {"A": (ga0, da0), "B": (gb0, db0), "C": (gc0, dc0)}, send0, recv0),
+    }.items():
+        copies = Copies(send, recv)
+        steps = scatter_steps(copies, 2, 1, functools.partial(terms, l), functools.partial(terms_dn, l), gu, dn, sgu, sdn, arrive, "")
+        next(steps)
+
+        def loads(l=l, gu=gu, dn=dn):
+            return ([pltpu.make_async_copy(terms(l, i).at[ALL, ALL, ALL, c], gu.at[i], sem_own.at[l, i]) for i in range(2)]
+                    + [pltpu.make_async_copy(terms_dn(l, 0).at[ALL, ALL, ALL, c], dn.at[0], sem_own.at[l, 2])])
+        runs[l] = (copies, steps, loads, gu, dn)
+
+    def begin(l):
+        copies, steps, loads, _, _ = runs[l]
+        for load in loads():
+            load.start()
+        next(steps)
+
+    def arrived(l):
+        for load in runs[l][2]():
+            load.wait()
+
+    def go(l, number):
+        for _ in range(number):
+            next(runs[l][1], None)
+
+    def inputs(step, slot, act):
+        l, f = 1 - step // TILES, lax.rem(step, TILES)
+        cols = pl.ds(pl.multiple_of(f * TILE, TILE), TILE)
+        copies = [(wgu.at[l, :, cols], wgu_t.at[slot, :, pl.ds(0, TILE)]), (wgu.at[2 + l, :, cols], wgu_t.at[slot, :, pl.ds(TILE, TILE)]), (wd.at[l, cols, :], wd_t.at[slot])]
+        for i, (src, dst) in enumerate(copies):
+            act(pltpu.make_async_copy(src, dst, sem_in.at[slot, i]))
+        for number, (gs, us) in ((1, (g1, u1)), (0, (g0, u0))):
+            @pl.when(l == number)
+            def _():
+                act(pltpu.make_async_copy(gs.at[:, cols], gate.at[slot], sem_in.at[slot, 3]))
+                act(pltpu.make_async_copy(us.at[:, cols], up.at[slot], sem_in.at[slot, 4]))
+
+    def outputs(step, act):
+        l, f = 1 - step // TILES, lax.rem(step, TILES)
+        cols = pl.ds(pl.multiple_of(f * TILE, TILE), TILE)
+        act(pltpu.make_async_copy(stage.at[:, pl.ds(0, TILE)], gus.at[l, :, cols], sem_out.at[0]))
+        act(pltpu.make_async_copy(stage.at[:, pl.ds(TILE, TILE)], gus.at[2 + l, :, cols], sem_out.at[1]))
+        act(pltpu.make_async_copy(stage_dn, dns.at[l, cols, :], sem_out.at[2]))
+
+    start, wait = (lambda copy: copy.start()), (lambda copy: copy.wait())
+    first = pltpu.make_async_copy(dy, ct, sem_h.at[0])
+    states = pltpu.make_async_copy(h1, hbuf, sem_h.at[1])
+    first.start()
+    states.start()
+    inputs(0, 0, start)
+    first.wait()
+
+    def body(step, _):
+        l, f, slot = 1 - step // TILES, lax.rem(step, TILES), lax.rem(step, 2)
+        inputs(step, slot, wait)
+
+        @pl.when(step + 1 < 2 * TILES)
+        def _():
+            inputs(step + 1, 1 - slot, start)
+
+        @pl.when(f == 0)
+        def _():
+            pltpu.make_async_copy(h1, hbuf, sem_h.at[1]).wait()
+
+            def norm(t, _):
+                rows = pl.ds(pl.multiple_of(t * 256, 256), 256)
+                wide = hbuf[rows, :].astype(F32)
+                n = wide * lax.rsqrt(jnp.mean(wide * wide, -1, keepdims=True) + 1e-6)
+                at[:, rows] = n.T.astype(BF16)
+                acc[rows, :] = jnp.zeros((256, D), F32)
+                return 0
+            lax.fori_loop(0, TOKENS // 256, norm, 0)
+
+        def hidden(t, _):
+            rows = pl.ds(pl.multiple_of(t * CHUNK, CHUNK), CHUNK)
+            by_p = dot(ct[rows, :], wd_t[slot], 1, 1).astype(BF16).astype(F32)
+            g, u = gate[slot, rows, :], up[slot, rows, :]
+            sig = 1.0 / (1.0 + jnp.exp(-g))
+            silu = g * sig
+            p[rows, :] = (silu * u).astype(BF16)
+            dgu[rows, pl.ds(TILE, TILE)] = (by_p * silu).astype(BF16)
+            dgu[rows, pl.ds(0, TILE)] = (by_p * u * (sig * (1.0 + g * (1.0 - sig)))).astype(BF16)
+            return 0
+        lax.fori_loop(0, CHUNKS, hidden, 0)
+
+        @pl.when(f > 0)
+        def _():
+            outputs(step - 1, wait)
+        stage_dn[...] = dot(p[...], ct[...], 0, 0).astype(BF16)
+
+        def weights(r, _):
+            rows = pl.ds(pl.multiple_of(r * 256, 256), 256)
+            stage[rows, :] = dot(at[rows, :], dgu[...], 1, 0).astype(BF16)
+            return 0
+        lax.fori_loop(0, D // 256, weights, 0)
+        outputs(step, start)
+
+        def states_back(t, _):
+            rows = pl.ds(pl.multiple_of(t * CHUNK, CHUNK), CHUNK)
+            acc[rows, :] += dot(dgu[rows, :], wgu_t[slot], 1, 1)
+            return 0
+        lax.fori_loop(0, CHUNKS, states_back, 0)
+
+        @pl.when(f == TILES - 1)
+        def _():
+            outputs(step, wait)
+
+            @pl.when(l == 1)
+            def _():
+                begin(1)
+
+            @pl.when(l == 0)
+            def _():
+                begin(0)
+
+            def norm_back(t, _):
+                rows = pl.ds(pl.multiple_of(t * 256, 256), 256)
+                wide = hbuf[rows, :].astype(F32)
+                s = lax.rsqrt(jnp.mean(wide * wide, -1, keepdims=True) + 1e-6)
+                n, by_a = wide * s, acc[rows, :]
+                by_h = s * (by_a - n * jnp.mean(by_a * n, -1, keepdims=True))
+                ct[rows, :] = (ct[rows, :].astype(F32) + by_h).astype(BF16)
+                return 0
+            lax.fori_loop(0, TOKENS // 256, norm_back, 0)
+
+            @pl.when(l == 1)
+            def _():
+                pltpu.make_async_copy(h0, hbuf, sem_h.at[1]).start()
+                arrived(1)
+
+        for i in range(TILES):
+            @pl.when(step == TILES + i)
+            def _():
+                go(1, EVENTS[i])
+        return 0
+
+    lax.fori_loop(0, 2 * TILES, body, 0)
+    last = pltpu.make_async_copy(ct, dx, sem_h.at[0])
+    last.start()
+    arrived(0)
+    go(1, 1000)
+    go(0, 1000)
+    ends = []
+    for l in (1, 0):
+        copies, _, _, gu, dn = runs[l]
+        for i in range(2):
+            ends.append(pltpu.make_async_copy(gu.at[i, x, y, z], gu_out.at[2 * i + l], sem_own.at[l, i]))
+        ends.append(pltpu.make_async_copy(dn.at[0, x, y, z], dn_out.at[l], sem_own.at[l, 2]))
+    for end in ends:
+        end.start()
+    for end in ends:
+        end.wait()
+    last.wait()
+    runs[1][0].finish()
+    runs[0][0].finish()
+
+
+EVENTS = (5, 5, 5, 5, 5, 5, 5)
+
+
+def back(dy, h0, h1, wgu, wd, g0, u0, g1, u1):
     hbm = pl.BlockSpec(memory_space=pl.ANY)
-    return pl.pallas_call(
-        functools.partial(scatter_kernel, M, N), name="scatter",
-        out_shape=(jax.ShapeDtypeStruct((M, 3, 8, FF), BF16), jax.ShapeDtypeStruct((N, 7, 8, D), BF16)),
-        in_specs=[hbm] * (M + N), out_specs=(hbm, hbm),
-        scratch_shapes=[*scatter_scratch(M, N), pltpu.SemaphoreType.DMA((SCATTER_COPIES,)), pltpu.SemaphoreType.DMA((SCATTER_COPIES,)), pltpu.SemaphoreType.DMA((M + N,))],
-        compiler_params=pltpu.CompilerParams(collective_id=number, has_side_effects=True, vmem_limit_bytes=60 * 1024 * 1024),
-    )(*gus, *dns)
-
-
-def dot(a, b, ca, cb):
-    return lax.dot_general(a, b, (((ca,), (cb,)), ((), ())), preferred_element_type=F32)
-
-
-def compute(x, dy, wg, wu, wd):
-    saved = []
-    h = x
-    for l in range(LAYERS):
-        wide = h.astype(F32)
-        s = lax.rsqrt(jnp.mean(wide**2, -1, keepdims=True) + 1e-6)
-        a = (wide * s).astype(BF16)
-        g, u = dot(a, wg[l], 1, 0), dot(a, wu[l], 1, 0)
-        p = (jax.nn.silu(g) * u).astype(BF16)
-        saved.append((h, s, a, g, u, p))
-        if l < LAYERS - 1:
-            h = h + dot(p, wd[l], 1, 0).astype(BF16)
-    ct, grads = dy, [None] * LAYERS
-    for l in reversed(range(LAYERS)):
-        h, s, a, g, u, p = saved[l]
-        by_down = dot(p, ct, 0, 0).astype(BF16)
-        by_p = dot(ct, wd[l], 1, 1).astype(BF16).astype(F32)
-        sig = jax.nn.sigmoid(g)
-        by_u = (by_p * g * sig).astype(BF16)
-        by_g = (by_p * u * (sig * (1 + g * (1 - sig)))).astype(BF16)
-        by_gate, by_up = dot(a, by_g, 0, 0).astype(BF16), dot(a, by_u, 0, 0).astype(BF16)
-        by_a = dot(by_g, wg[l], 1, 1) + dot(by_u, wu[l], 1, 1)
-        n = h.astype(F32) * s
-        ct = (ct.astype(F32) + s * (by_a - n * jnp.mean(by_a * n, -1, keepdims=True))).astype(BF16)
-        grads[l] = (by_gate, by_up, by_down)
-    return ct, grads
+    vmem, dma = pltpu.VMEM, pltpu.SemaphoreType.DMA
+    out = pl.pallas_call(
+        back_kernel, name="back",
+        out_shape=(jax.ShapeDtypeStruct((TOKENS, D), BF16), jax.ShapeDtypeStruct((4, 3, 8, FF), BF16), jax.ShapeDtypeStruct((2, 7, 8, D), BF16),
+                   jax.ShapeDtypeStruct((4, D, FF), BF16), jax.ShapeDtypeStruct((2, FF, D), BF16)),
+        in_specs=[hbm] * 9, out_specs=(hbm,) * 5,
+        scratch_shapes=[vmem((TOKENS, D), BF16), vmem((TOKENS, D), BF16), vmem((D, TOKENS), BF16), vmem((TOKENS, D), F32),
+                        vmem((2, TOKENS, TILE), F32), vmem((2, TOKENS, TILE), F32), vmem((2, D, 2 * TILE), BF16), vmem((2, TILE, D), BF16),
+                        vmem((TOKENS, TILE), BF16), vmem((TOKENS, 2 * TILE), BF16), vmem((D, 2 * TILE), BF16), vmem((TILE, D), BF16),
+                        *scatter_scratch(2, 1), *scatter_scratch(2, 1),
+                        *[dma((SCATTER_COPIES,))] * 4, dma((2, 5)), dma((2,)), dma((3,)), dma((2, 3))],
+        compiler_params=pltpu.CompilerParams(collective_id=1, has_side_effects=True, vmem_limit_bytes=63 * MIB),
+    )(dy, h0, h1, wgu, wd, g0, u0, g1, u1)
+    return out[:3]
+
+
+def normed(h):
+    wide = h.astype(F32)
+    return (wide * lax.rsqrt(jnp.mean(wide**2, -1, keepdims=True) + 1e-6)).astype(BF16)
 
 
 def solution(mesh):
@@ -420,12 +567,15 @@
         gu_in = jnp.concatenate([w_gate, w_up]).reshape(4, 3, 8, FF)
         gu, dn = gather(gu_in, w_down.reshape(2, 7, 8, D))
         gu, dn = gu.reshape(4, D, FF), dn.reshape(2, FF, D)
-        ct, grads = compute(x[0], dy[0], gu[:2], gu[2:], dn)
-        gus = [grads[l][i].reshape(*GRID, 3, 8, FF) for i in (0, 1) for l in (0, 1)]
-        dns = [grads[l][2].reshape(*GRID, 7, 8, D) for l in (0, 1)]
-        by_gu, by_dn = scatter(gus, dns)
+        x, dy = x[0], dy[0]
+        a = normed(x)
+        g0, u0 = dot(a, gu[0], 1, 0), dot(a, gu[2], 1, 0)
+        h = x + dot((jax.nn.silu(g0) * u0).astype(BF16), dn[0], 1, 0).astype(BF16)
+        a = normed(h)
+        g1, u1 = dot(a, gu[1], 1, 0), dot(a, gu[3], 1, 0)
+        dx, by_gu, by_dn = back(dy, x, h, gu, dn, g0, u0, g1, u1)
         by_gu = by_gu.reshape(4, 24, FF)
-        return ct[None], by_gu[:2], by_gu[2:], by_dn.reshape(2, 56, D)
+        return dx[None], by_gu[:2], by_gu[2:], by_dn.reshape(2, 56, D)
 
     rows = P(None, "dp", None)
     tokens = P(("rep", "dp"), None, None)

time: 403 us -> 348 us (0.86); the launches traced: 396 us -> 348 us
  matrix products: 189 us -> 53.1 us
  Pallas kernels: 172 us -> 275 us
  other arithmetic: 11 us -> 3.4 us
  local copies, waits for them, and re-layouts: 21.9 us -> 15.1 us
    dot_general x17 -> x5, matrix products: 189 us -> 53.1 us  [dot(): lax.dot_general(a, b, (((ca,), (cb,)), ((), ())), preferred_element_type=...]
    pallas_call x1, Pallas kernels: 96.7 us -> 200 us  [back(): pl.pallas_call(back_kernel, name='back', out_shape=(jax.ShapeDtypeStruct(...]
    unnamed x60 -> x14, local copies, waits for them, and re-layouts: 11.9 us -> 4.49 us
    convert_element_type x1 -> x0, other arithmetic: 5.68 us -> none  [compute(): (ct.astype(F32) + s * (by_a - n * jnp.mean(by_a * n, -1, keepdims=True)))...]
where the time goes in v2:
time: 348 us
  Pallas kernels  275 us (79%)
  matrix products  53.1 us (15%)
  local copies, waits for them, and re-layouts  15.1 us (4%)
    pallas_call x1, Pallas kernels, back(): pl.pallas_call(back_kernel, name='back', out_shape=(jax.ShapeDtypeStruct(...  200 us
    pallas_call x1, Pallas kernels, gather(): pl.pallas_call(gather_kernel, name='gather', out_shape=(jax.ShapeDtypeStr...  75.4 us
    dot_general x5, matrix products, dot(): lax.dot_general(a, b, (((ca,), (cb,)), ((), ())), preferred_element_type=...  53.1 us

profile of v2, /device:TPU:0, one launch (start us, length us, event | category | flops | bytes accessed | tf_op | source)
XLA Modules:
  0.0 347.6 jit_solution(3394053238002265224)
XLA Ops:
  0.6 0.0 copy-start.3
  0.6 0.0 copy-start.4
  0.7 2.6 multiply_reduce_fusion
  3.3 0.0 copy-done.3
  3.3 0.0 copy-done.4
  3.3 0.8 maximum_bitcast_fusion.gu_in
  4.1 75.4 %gather.1 = (bf16[4,2,2,4,2,3,8,1792]{7,6,5,4,3,2,1,0:T(8,128)(2,1)}, bf16[2,2,2,4,2,7,8,768]{7,6,5,4,3,2,1,0:T(8,128)(2,1)}) custom-call(bf16[4,3,8,1792]{3,2,1,0:T(8,128)(2,1)} %maximum_bitcast_fusion.gu_in, bf16[2,7,8,768]{3,2,1,0:T(8,128)(2,1)} %bitcast.39), custom_call_target="tpu_custom_call" | custom-call | tf_op jit(solution)/shard_map/gather/pallas_call | solution.py:198
  79.5 2.0 slice.34
  81.5 0.0 copy-start
  81.5 6.9 %fusion.15 = (bf16[1,2,2,4,2,3,8,1792]{7,6,5,4,3,2,1,0:T(8,128)(2,1)}, bf16[1,2,2,4,2,3,8,1792]{7,6,5,4,3,2,1,0:T(8,128)(2,1)}, bf16[1,2,2,4,2,3,8,1792]{7,6,5,4...) fusion(bf16[4,2,2,4,2,3,8,1792]{7,6,5,4,3,2,1,0:T(8,128)(2,1)} %get-tuple-element.9), kind=kLoop, calls=%fused_computation.21 | loop fusion | bytes 22020096 | tf_op jit(solution)/shard_map/slice | solution.py:575
  88.4 0.0 copy-done
  88.4 9.2 %fusion.6.u0 = f32[2048,1792]{1,0:T(8,128)} fusion(bf16[768,1792]{1,0:T(8,128)(2,1)S(1)} %bitcast.38, bf16[1,2048,768]{2,1,0:T(8,128)(2,1)S(1)} %copy-done, f32[2048]{0:T(1024)S(1)} %add_rsqrt_fusion.1), kind=kOutput, calls=%fused_computation.11 | convolution fusion | flops 5641863168 | bytes 20586496 | tf_op jit(solution)/shard_map/dot_general | solution.py:363
  97.7 9.1 %fusion.8.g0 = f32[2048,1792]{1,0:T(8,128)} fusion(bf16[768,1792]{1,0:T(8,128)(2,1)S(1)} %bitcast.37, bf16[1,2048,768]{2,1,0:T(8,128)(2,1)S(1)} %copy-done, f32[2048]{0:T(1024)S(1)} %add_rsqrt_fusion.1), kind=kOutput, calls=%fused_computation.12 | convolution fusion | flops 5641863168 | bytes 20586496 | tf_op jit(solution)/shard_map/dot_general | solution.py:363
  106.8 13.6 %fusion.1 = (f32[2048]{0:T(1024)S(1)}, bf16[2048,768]{1,0:T(8,128)(2,1)S(1)}) fusion(bf16[1792,768]{1,0:T(8,128)(2,1)S(1)} %bitcast.34, f32[2048,1792]{1,0:T(8,128)} %fusion.6.u0, f32[2048,1792]{1,0:T(8,128)} %fusion.8.g0, bf16[1,2048,768]{2,1,0:T(8,128)(2,1)S(1)} %copy-done), kind=kOutput, calls=%fused_computation.4 | convolution fusion | flops 5667026944 | bytes 38412288 | tf_op jit(solution)/shard_map/dot_general | solution.py:363
  120.4 0.0 copy-start.1
  120.4 0.0 copy-start.2
  120.4 12.1 %fusion.10.u1 = f32[2048,1792]{1,0:T(8,128)} fusion(bf16[768,1792]{1,0:T(8,128)(2,1)} %bitcast.36, bf16[2048,768]{1,0:T(8,128)(2,1)S(1)} %get-tuple-element.21.h1, f32[2048]{0:T(1024)S(1)} %add_rsqrt_fusion), kind=kOutput, calls=%fused_computation.13 | convolution fusion | flops 5641863168 | bytes 20586496 | tf_op jit(solution)/shard_map/dot_general | solution.py:363
  132.5 0.0 copy-done.1
  132.5 0.0 copy-done.2
  132.5 9.1 %fusion.12.g1 = f32[2048,1792]{1,0:T(8,128)} fusion(bf16[768,1792]{1,0:T(8,128)(2,1)S(1)} %bitcast.35, bf16[2048,768]{1,0:T(8,128)(2,1)S(1)} %get-tuple-element.21.h1, f32[2048]{0:T(1024)S(1)} %add_rsqrt_fusion), kind=kOutput, calls=%fused_computation.14 | convolution fusion | flops 5641863168 | bytes 20586496 | tf_op jit(solution)/shard_map/dot_general | solution.py:363
  141.6 199.7 %back.1 = (bf16[2048,768]{1,0:T(8,128)(2,1)}, bf16[4,3,8,1792]{3,2,1,0:T(8,128)(2,1)}, bf16[2,7,8,768]{3,2,1,0:T(8,128)(2,1)}, bf16[4,768,1792]{2,1,0:T(8,128)(2,1)}, bf16[2,1792,768]{2,1,0:T(8,128)(2,1)}) custom-call(bf16[2048,768]{1,0:T(8,128)(2,1)} %bitcast.32, bf16[2048,768]{1,0:T(8,128)(2,1)} %bitcast.30, bf16[2048,768]{1,0:T(8,128)(2,1)} %copy-done.1, ...), custom_call_target="tpu_custom_call" | custom-call | tf_op jit(solution)/shard_map/back/pallas_call | solution.py:545
  341.4 1.8 slice_bitcast_fusion
  343.1 0.0 copy-start.5
  343.1 3.8 %copy.13 = bf16[1,2048,768]{2,1,0:T(8,128)(2,1)} copy(bf16[1,2048,768]{2,1,0:T(8,128)(2,1)} %bitcast.33) | data formatting | bytes 6291456
  346.9 0.0 copy-done.5
  346.9 0.7 copy.14
  (2 shorter events, 0.0 us)
Async XLA Ops:
  0.6 2.7 copy-start.3
  0.6 2.7 copy-start.4
  81.5 7.0 %copy-start = (bf16[1,2048,768]{2,1,0:T(8,128)(2,1)S(1)}, bf16[1,2048,768]{2,1,0:T(8,128)(2,1)}, u32[]{:S(2)}) copy-start(bf16[1,2048,768]{2,1,0:T(8,128)(2,1)} %param.5) | copy-start | bytes 9437188
  120.4 12.2 %copy-start.1 = (bf16[2048,768]{1,0:T(8,128)(2,1)}, bf16[2048,768]{1,0:T(8,128)(2,1)S(1)}, u32[]{:S(2)}) copy-start(bf16[2048,768]{1,0:T(8,128)(2,1)S(1)} %get-tuple-element.21.h1) | copy-start | bytes 9437188
  120.4 12.1 %copy-start.2 = (bf16[1,2,2,4,2,3,8,1792]{7,6,5,4,3,2,1,0:T(8,128)(2,1)S(1)}, bf16[1,2,2,4,2,3,8,1792]{7,6,5,4,3,2,1,0:T(8,128)(2,1)}, u32[]{:S(2)}) copy-start(bf16[1,2,2,4,2,3,8,1792]{7,6,5,4,3,2,1,0:T(8,128)(2,1)} %get-tuple-element.15) | copy-start | bytes 8257540
  343.1 3.8 %copy-start.5 = (bf16[2,7,8,768]{3,2,1,0:T(8,128)(2,1)S(1)}, bf16[2,7,8,768]{3,2,1,0:T(8,128)(2,1)}, u32[]{:S(2)}) copy-start(bf16[2,7,8,768]{3,2,1,0:T(8,128)(2,1)} %get-tuple-element.13) | copy-start | bytes 516100

commit v3 on v0

v3 whole, which is shorter than its diff:
```python
import jax
import jax.numpy as jnp
from jax import lax
from jax.experimental import pallas as pl
from jax.experimental.pallas import tpu as pltpu
from jax.sharding import PartitionSpec as P

F32 = jnp.float32
BF16 = jnp.bfloat16
LAYERS, TOKENS, D, FF = 2, 2048, 768, 1792
NX, NY, NZ, NC = GRID = (2, 2, 4, 2)
ROWS = 8
GU_UNITS = {"A": (0, 1), "C": (1, 1), "B": (2, 1), "AC": (0, 2), "all": 3}
DN_UNITS = {"A": (0, 2), "C": (2, 2), "B": (4, 3), "AC": (0, 4), "all": 7}
ALL = slice(None)
YES, NO = True, False
MESH = pl.DeviceIdType.MESH
CHIPS = NX * NY * NZ
ARRIVALS = CHIPS - 1
TILE = 256
TILES = FF // TILE
EPS = 1e-6
LIMIT = 63 * 2**20


def place():
    me = lax.axis_index("dp")
    return me // (NC * NZ * NY), lax.rem(me // (NC * NZ), NY), lax.rem(me // NC, NZ), lax.rem(me, NC)


def index(x, y, z, c):
    return ((x * NY + y) * NZ + z) * NC + c


def after(z):
    return lax.rem(2 * z + 1, 5)


def before(z):
    return lax.rem(3 * z + 2, 5)


def partners():
    x, y, z, c = place()
    return {"x": index(1 - x, y, z, c), "y": index(x, 1 - y, z, c), "z": index(x, y, after(z), c), "c": index(x, y, z, 1 - c)}


def greet():
    x, y, z, c = place()
    barrier = pltpu.get_barrier_semaphore()
    others = [*partners().values(), index(x, y, before(z), c)]
    for other in others:
        pl.semaphore_signal(barrier, inc=1, device_id={"dp": other}, device_id_type=MESH)
    pl.semaphore_wait(barrier, len(others))


def rings():
    ring = [place()[2]]
    while len(ring) < NZ:
        ring.append(before(ring[-1]))
    return ring


class Copies:
    def __init__(self, send, recv, to):
        self.send, self.recv, self.to, self.made, self.number = send, recv, to, {}, {}

    def copy(self, src, dst, lane, name, way):
        number = self.number.setdefault(name, len(self.number))
        return pltpu.make_async_remote_copy(src_ref=src, dst_ref=dst, send_sem=self.send.at[lane], recv_sem=self.recv.at[number], device_id={"dp": self.to[way]}, device_id_type=MESH)

    def start(self, name, pair, way, lane, together=None):
        self.made[name] = (pair, way, lane)
        src, dst = pair()
        self.copy(src, dst, lane, together or name, way).start()

    def wait(self, name):
        pair, way, lane = self.made[name]
        src, dst = pair()
        self.copy(src, dst, lane, name, way).wait_recv()

    def wait_together(self, name, whole, way, lane):
        self.copy(whole, whole, lane, name, way).wait_recv()

    def finish(self, whole, way, lane):
        self.copy(whole, whole, lane, next(iter(self.number)), way).wait_send()


def gather_steps(copies, source, target, units, first, number):
    x, y, z, c = place()
    X, Y = 1 - x, 1 - y
    ring = rings()
    wire, die = range(2)

    def at():
        return pl.ds(first, number)

    def rows(colour):
        return pl.ds(*units[colour])

    def region(colour, xs, ys, k):
        return target.at[at(), xs, ys, ring[k], c, rows(colour)]

    def send(name, way, colour, xs, ys, k, mine=NO):
        copies.start(colour + name, lambda: (source.at[at(), rows(colour)] if mine else region(colour, xs, ys, k), region(colour, xs, ys, k)), way, wire)

    def share(colour, xs, ys, k):
        copies.start(f"s{len(copies.made)}", lambda: (region(colour, xs, ys, k), region(colour, xs, ys, k)), "c", die, "die")

    yield
    send("x", "x", "C", x, y, 0, YES)
    send("y", "y", "B", x, y, 0, YES)
    send("z1", "z", "A", x, y, 0, YES)
    send("x0", "x", "A", x, y, 0, YES)
    send("y0", "y", "A", x, y, 0, YES)
    copies.start("own", lambda: (source.at[at()], target.at[at(), x, y, z, c]), "c", die, "die")
    yield
    copies.wait("Cx")
    send("z1", "z", "C", ALL, y, 0)
    send("y0", "y", "C", ALL, y, 0)
    share("C", X, y, 0)
    yield
    copies.wait("By")
    send("z1", "z", "B", x, ALL, 0)
    send("x0", "x", "B", x, ALL, 0)
    share("B", x, Y, 0)
    for k in range(1, NZ):
        on = k < NZ - 1
        yield
        copies.wait(f"Az{k}")
        if on:
            send(f"z{k + 1}", "z", "A", x, y, k)
        send(f"x{k}", "x", "A", x, y, k)
        send(f"y{k}", "y", "A", x, y, k)
        share("A", x, y, k)
        yield
        copies.wait(f"Ax{k - 1}")
        send(f"Y{k - 1}", "y", "A", X, y, k - 1)
        share("A", X, y, k - 1)
        yield
        copies.wait(f"Cz{k}")
        if on:
            send(f"z{k + 1}", "z", "C", ALL, y, k)
        send(f"y{k}", "y", "C", ALL, y, k)
        share("C", ALL, y, k)
        yield
        copies.wait(f"Bz{k}")
        if on:
            send(f"z{k + 1}", "z", "B", x, ALL, k)
        send(f"x{k}", "x", "B", x, ALL, k)
        share("B", x, ALL, k)
    yield
    copies.wait(f"Ax{k}")
    send(f"Y{k}", "y", "A", X, y, k)
    share("A", X, y, k)
    for k in range(NZ):
        yield
        copies.wait(f"Bx{k}")
        share("B", X, ALL, k)
        yield
        copies.wait(f"Cy{k}")
        share("C", ALL, Y, k)
        yield
        copies.wait(f"Ay{k}")
        copies.wait(f"AY{k}")
        share("A", ALL, Y, k)
    yield
    flat = target.reshape(target.shape[0], CHIPS * NC, *target.shape[-3:])
    copies.wait_together("die", flat.at[at(), pl.ds(0, CHIPS)], "c", die)
    copies.finish(flat.at[at(), pl.ds(0, CHIPS)], "c", die)
    copies.finish(flat.at[at(), pl.ds(0, ARRIVALS)], "x", wire)


def add_pairs(dst, src, count, pairs):
    def body(m, _):
        for i, j in pairs:
            dst[(m, *i)] = (dst[(m, *i)].astype(F32) + src[(m, *j)].astype(F32)).astype(BF16)
        return 0
    lax.fori_loop(0, count, body, 0)


def scatter_steps(copies, count, terms, which, total, other, arrive, units):
    x, y, z, c = place()
    X, Y = 1 - x, 1 - y
    ring = rings()
    away = 1 - c
    slots, used = {}, dict.fromkeys("ABC", 0)
    lanes = {"A": 0, "B": 1, "C": 2, "die": 3}

    def half(colour, far):
        if colour == "B":
            return (X if far else x), ALL
        return ALL, (Y if far else y)

    def blocks(xs, ys):
        return [(e, ys) for e in range(NX)] if xs is ALL else [(xs, e) for e in range(NY)] if ys is ALL else [(xs, ys)]

    def swap(k, far):
        for colour in ("AC", "B"):
            def pair(colour=colour):
                xs, ys = half(colour, far)
                rows = pl.ds(*units[colour])
                return terms().at[which, xs, ys, ring[k], away, rows], other.at[ALL, xs, ys, ring[k], rows]
            copies.start(f"s{colour}{k}{far}", pair, "c", lanes["die"])

    def swapped(k, far):
        for colour in ("AC", "B"):
            copies.wait(f"s{colour}{k}{far}")
            a, n = units[colour]
            at = [(bx, by, ring[k], a + u) for bx, by in blocks(*half(colour, far)) for u in range(n)]
            add_pairs(total, other, count, [(i, i) for i in at])

    def send(name, way, colour, xs, ys, k):
        number, at = len(blocks(xs, ys)), used[colour]
        used[colour] += number
        slots[colour + name] = at

        def pair():
            return total.at[ALL, xs, ys, ring[k], pl.ds(*units[colour])], arrive[colour].at[ALL, pl.ds(at, number) if number > 1 else at]
        copies.start(colour + name, pair, way, lanes[colour])

    def take(name, colour, xs, ys, k):
        copies.wait(colour + name)
        (a, n), at = units[colour], slots[colour + name]
        add_pairs(total, arrive[colour], count, [((bx, by, ring[k], a + u), (at + e, u)) for e, (bx, by) in enumerate(blocks(xs, ys)) for u in range(n)])

    def far(k):
        swapped(k, YES)
        send(f"y{k}", "y", "A", ALL, Y, k)
        send(f"y{k}", "y", "C", ALL, Y, k)
        send(f"x{k}", "x", "B", X, ALL, k)

    def chain(colour, xs, ys, k):
        t = k or NZ
        if t > 1:
            take(f"z{t - 1}", colour, xs, ys, k)
        if t < NZ:
            send(f"z{t}", "z", colour, xs, ys, k)

    def second(k):
        take(f"y{k}", "A", ALL, y, k)
        send(f"x{k}", "x", "A", X, y, k)
        yield
        take(f"y{k}", "C", ALL, y, k)
        chain("C", ALL, y, k)
        if k == 0:
            send("x", "x", "C", X, y, k)
        yield
        take(f"x{k}", "B", x, ALL, k)
        chain("B", x, ALL, k)
        if k == 0:
            send("y", "y", "B", x, Y, k)

    def third(k):
        take(f"x{k}", "A", x, y, k)
        chain("A", x, y, k)

    order = [*range(1, NZ), 0]
    yield
    for k, distant in ((1, YES), (2, YES), (1, NO), (3, YES), (2, NO), (0, YES), (3, NO), (0, NO)):
        swap(k, distant)
    yield
    far(order[0])
    yield
    far(order[1])
    for at, k in enumerate(order):
        yield
        swapped(k, NO)
        if at:
            yield
            third(order[at - 1])
        yield
        yield from second(k)
        if at + 2 < NZ:
            yield
            far(order[at + 2])
    yield
    third(0)
    yield
    take("x", "C", x, y, 0)
    yield
    take("y", "B", x, y, 0)
    copies.finish(other, "c", lanes["die"])
    for colour in "ABC":
        copies.finish(arrive[colour], "x", lanes[colour])


class Clock:
    def __init__(self, runs):
        self.runs, self.on, self.done = runs, {}, {}
        for run in runs:
            next(run)

    def launch(self, i, begin, length):
        self.on[i] = (begin, length)
        self.done[i] = 0

    def due(self):
        return [(begin + length * self.done[i] / 29, i) for i, (begin, length) in self.on.items()]

    def step(self, i):
        self.done[i] += 1
        if next(self.runs[i], "end") == "end":
            del self.on[i]

    def advance(self, until):
        while self.on and min(self.due())[0] <= until:
            self.step(min(self.due())[1])

    def finish(self, i):
        while i in self.on:
            self.step(min(self.due())[1])


def nn(a, b):
    return jnp.dot(a, b, preferred_element_type=F32)


def nt(a, b):
    return lax.dot_general(a, b, (((1,), (1,)), ((), ())), preferred_element_type=F32)


def span(i, n):
    return pl.ds(pl.multiple_of(i * n, n), n)


def scale_of(wide):
    return lax.rsqrt(jnp.mean(wide * wide, -1, keepdims=True) + EPS)


def start(copy):
    copy.start()


def wait(copy):
    copy.wait()


def repeat(number, body):
    def one(i, _):
        body(i)
        return 0
    lax.fori_loop(0, number, one, 0)


FORWARD_TIMES = ((0, 26), (12, 20), (22, 30), (44, 20))
TILE_CLOCKS = ((27, 2.5), (58, 2.5))
DOWN_CLOCK = (45, 2)
WIDE = 512


def forward_kernel(x, gu_in, dn_in, gu, dn, h1, silu, slope, pt, h, a, p, wgu_t, wd, silu_t, slope_t, pt_t, gu_own, dn_own, send, recv, sem_in, sem_out, sem_h, local):
    greet()
    mx, my, mz, mc = place()
    to = partners()
    clock = Clock([gather_steps(Copies(send.at[2 * l + i], recv.at[2 * l + i], to), *which, (2 - i) * l, 2 - i)
                   for l in range(LAYERS) for i, which in enumerate(((gu_in, gu, GU_UNITS), (dn_in, dn, DN_UNITS)))])
    for i, times in enumerate(FORWARD_TIMES):
        clock.launch(i, *times)

    def mine(act, back):
        ways = [(gu_own, gu.at[ALL, mx, my, mz, mc]), (dn_own, dn.at[ALL, mx, my, mz, mc])] if back else [(gu_in, gu_own), (dn_in, dn_own)]
        for i, (src, dst) in enumerate(ways):
            act(pltpu.make_async_copy(src, dst, local.at[2 * back + i]))

    mine(start, 0)
    states = pltpu.make_async_copy(x, h, sem_h.at[0])
    states.start()
    clock.advance(0)
    mine(wait, 0)
    mine(start, 1)
    states.wait()
    mine(wait, 1)

    @pl.loop(0, TOKENS // TILE)
    def norm(t):
        wide = h[span(t, TILE), :].astype(F32)
        a[span(t, TILE), :] = (wide * scale_of(wide)).astype(BF16)

    clock.finish(0)

    def inputs(l, f, slot, act):
        for i in range(2):
            act(pltpu.make_async_copy(gu.at[2 * l + i].reshape(D, FF).at[:, span(f, TILE)], wgu_t.at[slot, :, pl.ds(i * TILE, TILE)], sem_in.at[slot, i]))

    def outputs(l, f, slot, act):
        act(pltpu.make_async_copy(silu_t.at[slot], silu.at[l, f], sem_out.at[slot, 0]))
        act(pltpu.make_async_copy(slope_t.at[slot], slope.at[l, f], sem_out.at[slot, 1]))
        act(pltpu.make_async_copy(pt_t.at[slot], pt.at[l, span(f, TILE), :], sem_out.at[slot, 2]))

    def hidden(l):
        inputs(l, 0, 0, start)

        def tile(f):
            slot = lax.rem(f, 2)
            inputs(l, f, slot, wait)

            @pl.when(f + 1 < TILES)
            def _():
                inputs(l, f + 1, 1 - slot, start)

            @pl.when(f > 1)
            def _():
                outputs(l, f - 2, slot, wait)

            for t in range(TOKENS // TILE):
                rows = pl.ds(t * TILE, TILE)
                both = nn(a[rows, :], wgu_t[slot])
                g, u = both[:, :TILE], both[:, TILE:]
                sig = 0.5 * jnp.tanh(0.5 * g) + 0.5
                s = g * sig
                out = s * u
                silu_t[slot, rows, :] = s
                slope_t[slot, rows, :] = u * (sig + s * (1.0 - sig))
                pt_t[slot, :, rows] = out.T.astype(BF16)
                if l == 0:
                    p[rows, span(f, TILE)] = out.astype(BF16)
            outputs(l, f, slot, start)
            for i in range(TILES):
                @pl.when(f == i)
                def _():
                    clock.advance(TILE_CLOCKS[l][0] + (i + 1) * TILE_CLOCKS[l][1])
        repeat(TILES, tile)
        for f in (TILES - 2, TILES - 1):
            outputs(l, f, f % 2, wait)

    hidden(0)
    clock.finish(1)
    down = pltpu.make_async_copy(dn.at[0].reshape(FF, D), wd, sem_h.at[1])
    down.start()
    down.wait()

    def second(t):
        rows = span(t, WIDE)
        new = (h[rows, :].astype(F32) + nn(p[rows, :], wd[ALL, ALL]).astype(BF16).astype(F32)).astype(BF16)
        h[rows, :] = new
        wide = new.astype(F32)
        a[rows, :] = (wide * scale_of(wide)).astype(BF16)
        for i in range(TOKENS // WIDE):
            @pl.when(t == i)
            def _():
                clock.advance(DOWN_CLOCK[0] + (i + 1) * DOWN_CLOCK[1])
    repeat(TOKENS // WIDE, second)
    states = pltpu.make_async_copy(h, h1, sem_h.at[0])
    states.start()
    clock.finish(2)
    hidden(1)
    clock.finish(3)
    states.wait()


GATHER_RECV = 32


def forward(x, gu_in, dn_in):
    hbm = pl.BlockSpec(memory_space=pl.ANY)
    vmem, dma = pltpu.VMEM, pltpu.SemaphoreType.DMA
    wide = jax.ShapeDtypeStruct((LAYERS, TILES, TOKENS, TILE), F32)
    double = vmem((2, TOKENS, TILE), F32)
    return pl.pallas_call(
        forward_kernel, name="forward",
        out_shape=(jax.ShapeDtypeStruct((2 * LAYERS, *GRID, *gu_in.shape[1:]), BF16), jax.ShapeDtypeStruct((LAYERS, *GRID, *dn_in.shape[1:]), BF16),
                   jax.ShapeDtypeStruct((TOKENS, D), BF16), wide, wide, jax.ShapeDtypeStruct((LAYERS, FF, TOKENS), BF16)),
        in_specs=[hbm] * 3, out_specs=(hbm,) * 6,
        scratch_shapes=[vmem((TOKENS, D), BF16), vmem((TOKENS, D), BF16), vmem((TOKENS, FF), BF16), vmem((2, D, 2 * TILE), BF16), vmem((FF, D), BF16),
                        double, double, vmem((2, TILE, TOKENS), BF16), vmem(gu_in.shape, BF16), vmem(dn_in.shape, BF16),
                        dma((2 * LAYERS, 2)), dma((2 * LAYERS, GATHER_RECV)), dma((2, 2)), dma((2, 3)), dma((2,)), dma((4,))],
        compiler_params=pltpu.CompilerParams(collective_id=0, has_side_effects=YES, vmem_limit_bytes=LIMIT),
    )(x, gu_in, dn_in)


BACK_TIMES = ((45, 26), (58, 16), (67, 24), (76, 16))
GRADS_CLOCK = (46, 3)
LATE_DOWN_CLOCK = (67, 1)
LATE_STATES_CLOCK = (74, 2)


def back_kernel(dy, h0, h1, wgu, wd, silu, slope, pt, dx, gu_out, dn_out, gus, dns, late,
                ct, hbuf, at, acc, gate, up, wgu_t, wd_t, p, dgu, stage, stage_dn,
                gu1, gx1, ga1, gb1, gc1, dn1, dx1, da1, db1, dc1, gu0, gx0, ga0, gb0, gc0, dn0, dx0, da0, db0, dc0,
                send, recv, sem_in, sem_h, sem_out, sem_late, sem_own):
    greet()
    to = partners()
    mx, my, mz, mc = place()
    collect = []
    for l, sets in ((1, ((gu1, gx1, ga1, gb1, gc1), (dn1, dx1, da1, db1, dc1))), (0, ((gu0, gx0, ga0, gb0, gc0), (dn0, dx0, da0, db0, dc0)))):
        for i, (total, other, *slots) in enumerate(sets):
            def terms(l=l, i=i):
                return dns.reshape(LAYERS, *GRID, DN_UNITS["all"], ROWS, D) if i else gus.reshape(2 * LAYERS, *GRID, GU_UNITS["all"], ROWS, FF)

            which = pl.ds(l, 1) if i else pl.ds(2 * l, 2)

            def own(total=total, terms=terms, which=which, number=len(collect)):
                return pltpu.make_async_copy(terms().at[which, ALL, ALL, ALL, mc], total, sem_own.at[number])

            def away(total=total, l=l, i=i, number=len(collect)):
                here = total.at[ALL, mx, my, mz]
                return pltpu.make_async_copy(here, dn_out.at[pl.ds(l, 1)] if i else gu_out.at[pl.ds(2 * l, 2)], sem_own.at[number])
            n = len(collect)
            steps = scatter_steps(Copies(send.at[n], recv.at[n], to), 2 - i, terms, which, total, other, dict(zip("ABC", slots)), DN_UNITS if i else GU_UNITS)
            collect.append((steps, own, away))
    clock = Clock([one[0] for one in collect])

    def launch(i):
        collect[i][1]().start()
        clock.launch(i, *BACK_TIMES[i])
        clock.step(i)

    def ready(i):
        collect[i][1]().wait()

    def inputs(step, slot, act):
        l, f = 1 - step // TILES, lax.rem(step, TILES)
        cols = span(f, TILE)
        copies = [(wgu.at[2 * l, :, cols], wgu_t.at[slot, :, pl.ds(0, TILE)]), (wgu.at[2 * l + 1, :, cols], wgu_t.at[slot, :, pl.ds(TILE, TILE)]),
                  (wd.at[l, cols, :], wd_t.at[slot]), (silu.at[l, f], gate.at[slot]), (slope.at[l, f], up.at[slot]), (pt.at[l, cols, :], p.at[slot])]
        for i, (src, dst) in enumerate(copies):
            act(pltpu.make_async_copy(src, dst, sem_in.at[slot, i]))

    def outputs(l, f, act):
        act(pltpu.make_async_copy(stage.at[:, pl.ds(0, TILE)], gus.at[2 * l, :, span(f, TILE)], sem_out.at[0]))
        act(pltpu.make_async_copy(stage.at[:, pl.ds(TILE, TILE)], gus.at[2 * l + 1, :, span(f, TILE)], sem_out.at[1]))

    def down_output(l, f, act):
        act(pltpu.make_async_copy(stage_dn, dns.at[l, span(f, TILE), :], sem_out.at[2]))

    def late_copy(f, slot, act, back):
        ends = (late.at[f], dgu.at[slot]) if back else (dgu.at[slot], late.at[f])
        act(pltpu.make_async_copy(*ends, sem_late.at[slot]))

    def states_back(slot):
        half = TOKENS // 2

        @pl.loop(0, 2)
        def _(t):
            acc[span(t, half), :] += nt(dgu[slot, span(t, half), :], wgu_t[slot])

    def norm_back():
        @pl.loop(0, TOKENS // TILE)
        def _(t):
            rows = span(t, TILE)
            wide = hbuf[rows, :].astype(F32)
            s = scale_of(wide)
            n, by_a = wide * s, acc[rows, :]
            by_h = s * (by_a - n * jnp.mean(by_a * n, -1, keepdims=True))
            ct[rows, :] = (ct[rows, :].astype(F32) + by_h).astype(BF16)

    first = pltpu.make_async_copy(dy, ct, sem_h.at[0])
    first.start()
    pltpu.make_async_copy(h1, hbuf, sem_h.at[1]).start()
    inputs(0, 0, start)
    first.wait()

    def body(step):
        l, f, slot = 1 - step // TILES, lax.rem(step, TILES), lax.rem(step, 2)
        inputs(step, slot, wait)

        @pl.when(step + 1 < 2 * TILES)
        def _():
            inputs(step + 1, 1 - slot, start)

        @pl.when(f == 0)
        def _():
            pltpu.make_async_copy(h1, hbuf, sem_h.at[1]).wait()

            @pl.loop(0, TOKENS // TILE)
            def _(t):
                rows = span(t, TILE)
                wide = hbuf[rows, :].astype(F32)
                at[:, rows] = (wide * scale_of(wide)).T.astype(BF16)
                acc[rows, :] = jnp.zeros((TILE, D), F32)

        @pl.when(step > TILES + 1)
        def _():
            late_copy(f - 2, slot, wait, NO)

        @pl.loop(0, 2)
        def _(t):
            rows = span(t, TOKENS // 2)
            by_p = nt(ct[rows, :], wd_t[slot]).astype(BF16).astype(F32)
            dgu[slot, rows, pl.ds(0, TILE)] = (by_p * up[slot, rows, :]).astype(BF16)
            dgu[slot, rows, pl.ds(TILE, TILE)] = (by_p * gate[slot, rows, :]).astype(BF16)

        @pl.when(f > 0)
        def _():
            outputs(l, f - 1, wait)
        stage[ALL, ALL] = nn(at[ALL, ALL], dgu[slot]).astype(BF16)
        outputs(l, f, start)

        @pl.when(l == 0)
        def _():
            late_copy(f, slot, start, NO)

        @pl.when(l == 1)
        def _():
            @pl.when(f > 0)
            def _():
                down_output(l, f - 1, wait)
            stage_dn[ALL, ALL] = nn(p[slot], ct[ALL, ALL]).astype(BF16)
            down_output(l, f, start)
            states_back(slot)

        @pl.when(step == TILES - 1)
        def _():
            outputs(l, f, wait)
            launch(0)
            down_output(l, f, wait)
            launch(1)
            norm_back()
            pltpu.make_async_copy(h0, hbuf, sem_h.at[1]).start()
            ready(0)
            ready(1)

        for i in range(TILES):
            @pl.when(step == TILES + i)
            def _():
                clock.advance(GRADS_CLOCK[0] + (i + 1) * GRADS_CLOCK[1])

    repeat(2 * TILES, body)
    outputs(0, TILES - 1, wait)
    launch(2)
    for f in (TILES - 2, TILES - 1):
        late_copy(f, (f + TILES) % 2, wait, NO)

    def again(f, slot, act, which):
        if which:
            late_copy(f, slot, act, YES)
            for i in range(2):
                act(pltpu.make_async_copy(wgu.at[i, :, span(f, TILE)], wgu_t.at[slot, :, pl.ds(i * TILE, TILE)], sem_in.at[slot, i]))
        else:
            act(pltpu.make_async_copy(pt.at[0, span(f, TILE), :], p.at[slot], sem_in.at[slot, 2]))

    again(0, 0, start, NO)
    again(0, 0, start, YES)
    ready(2)

    def late_down(f):
        slot = lax.rem(f, 2)
        again(f, slot, wait, NO)

        @pl.when(f + 1 < TILES)
        def _():
            again(f + 1, 1 - slot, start, NO)

        @pl.when(f > 0)
        def _():
            down_output(0, f - 1, wait)
        stage_dn[ALL, ALL] = nn(p[slot], ct[ALL, ALL]).astype(BF16)
        down_output(0, f, start)
        for i in range(TILES):
            @pl.when(f == i)
            def _():
                clock.advance(LATE_DOWN_CLOCK[0] + (i + 1) * LATE_DOWN_CLOCK[1])
    repeat(TILES, late_down)
    down_output(0, TILES - 1, wait)
    launch(3)

    def late_states(f):
        slot = lax.rem(f, 2)
        again(f, slot, wait, YES)

        @pl.when(f + 1 < TILES)
        def _():
            again(f + 1, 1 - slot, start, YES)
        states_back(slot)

        @pl.when(f == 0)
        def _():
            ready(3)
        for i in range(TILES):
            @pl.when(f == i)
            def _():
                clock.advance(LATE_STATES_CLOCK[0] + (i + 1) * LATE_STATES_CLOCK[1])
    repeat(TILES, late_states)
    norm_back()
    last = pltpu.make_async_copy(ct, dx, sem_h.at[0])
    last.start()
    for i in range(len(collect)):
        clock.finish(i)
    for act in (start, wait):
        for one in collect:
            act(one[-1]())
    last.wait()


SCATTER_RECV = 43


def back(dy, h0, h1, wgu, wd, silu, slope, pt):
    hbm = pl.BlockSpec(memory_space=pl.ANY)
    vmem, dma = pltpu.VMEM, pltpu.SemaphoreType.DMA
    buffers = []
    for count, units, columns in ((2, GU_UNITS, FF), (1, DN_UNITS, D)):
        whole = vmem((count, NX, NY, NZ, units["all"], ROWS, columns), BF16)
        buffers += [whole, whole, *(vmem((count, ARRIVALS, units[colour][1], ROWS, columns), BF16) for colour in "ABC")]
    double, states = vmem((2, TOKENS, TILE), F32), vmem((TOKENS, D), BF16)
    return pl.pallas_call(
        back_kernel, name="back",
        out_shape=(jax.ShapeDtypeStruct((TOKENS, D), BF16), jax.ShapeDtypeStruct((2 * LAYERS, GU_UNITS["all"], ROWS, FF), BF16),
                   jax.ShapeDtypeStruct((LAYERS, DN_UNITS["all"], ROWS, D), BF16), jax.ShapeDtypeStruct((2 * LAYERS, D, FF), BF16),
                   jax.ShapeDtypeStruct((LAYERS, FF, D), BF16), jax.ShapeDtypeStruct((TILES, TOKENS, 2 * TILE), BF16)),
        in_specs=[hbm] * 8, out_specs=(hbm,) * 6,
        scratch_shapes=[states, states, vmem((D, TOKENS), BF16), vmem((TOKENS, D), F32), double, double, vmem((2, D, 2 * TILE), BF16), vmem((2, TILE, D), BF16),
                        vmem((2, TILE, TOKENS), BF16), vmem((2, TOKENS, 2 * TILE), BF16), vmem((D, 2 * TILE), BF16), vmem((TILE, D), BF16), *buffers, *buffers,
                        dma((4, 4)), dma((4, SCATTER_RECV)), dma((2, 6)), dma((2,)), dma((3,)), dma((2,)), dma((4,))],
        compiler_params=pltpu.CompilerParams(collective_id=1, has_side_effects=YES, vmem_limit_bytes=LIMIT),
    )(dy, h0, h1, wgu, wd, silu, slope, pt)[:3]


def solution(mesh):
    def step(x, dy, w_gate, w_up, w_down):
        gu_in = jnp.stack([w_gate, w_up], 1).reshape(2 * LAYERS, GU_UNITS["all"], ROWS, FF)
        x, dy = x[0], dy[0]
        gu, dn, h, silu, slope, pt = forward(x, gu_in, w_down.reshape(LAYERS, DN_UNITS["all"], ROWS, D))
        dx, by_gu, by_dn = back(dy, x, h, gu.reshape(2 * LAYERS, D, FF), dn.reshape(LAYERS, FF, D), silu, slope, pt)
        by_gu = by_gu.reshape(w_gate.shape[0], 2, *w_gate.shape[1:])
        return dx[None], by_gu[:, 0], by_gu[:, 1], by_dn.reshape(w_down.shape)

    rows = P(None, "dp", None)
    tokens, grads = P(("rep", "dp"), None, None), P("rep", "dp", None)
    return jax.shard_map(step, mesh=mesh, in_specs=(tokens, tokens, rows, rows, rows), out_specs=(tokens, grads, grads, grads), check_vma=NO)
```

time: 1660 us -> 270 us (0.16); the launches traced: 1640 us -> 270 us
  starting transfers between devices: 554 us -> 0 us
  matrix products: 495 us -> 0 us
  other arithmetic: 294 us -> 1.04 us
  Pallas kernels: 0 us -> 261 us
  waiting for transfers between devices: 183 us -> 0 us
  local copies, waits for them, and re-layouts: 95.3 us -> 6.97 us
    dot_general x231 -> x0, starting transfers between devices: 554 us -> none  [the longest x99 212 us: matmul(): jnp.dot(a, w, preferred_element_type=jnp.float32).astype(jnp.bfloat16)]
    dot_general x122 -> x0, matrix products: 495 us -> none  [the longest x36 189 us: layer(): up = jnp.dot(a, w['w_up'], preferred_element_type=jnp.float32)]
    pallas_call x0 -> x2, Pallas kernels: none -> 261 us  [the longest x1 148 us: back(): pl.pallas_call(back_kernel, name='back', out_shape=(jax.ShapeDtypeStruct(...]
    dot_general x192 -> x0, other arithmetic: 260 us -> none
    dot_general x231 -> x0, waiting for transfers between devices: 157 us -> none  [the longest x99 150 us: matmul(): jnp.dot(a, w, preferred_element_type=jnp.float32).astype(jnp.bfloat16)]
    dot_general x66 -> x0, local copies, waits for them, and re-layouts: 51.8 us -> none  [the longest x34 51.8 us: matmul(): jnp.dot(a, w, preferred_element_type=jnp.float32).astype(jnp.bfloat16)]
    unnamed x56 -> x4, local copies, waits for them, and re-layouts: 38.6 us -> 4.43 us
    squeeze x5 -> x0, waiting for transfers between devices: 25.8 us -> none  [stack(): h = layer(h, {name: w[number] for name, w in weights.items()})]
  transfers between devices with their start and end apart: 236 -> 0, of which waited for: 74 -> 0; matrix products, arithmetic and copies ran while one was open for 51% -> 0% of each run, Pallas kernels for 0% -> 0%
where the time goes in v3:
time: 270 us
  Pallas kernels  261 us (97%)
  local copies, waits for them, and re-layouts  6.97 us (3%)
    pallas_call x1, Pallas kernels, back(): pl.pallas_call(back_kernel, name='back', out_shape=(jax.ShapeDtypeStruct(...  148 us
    pallas_call x1, Pallas kernels, forward(): pl.pallas_call(forward_kernel, name='forward', out_shape=(jax.ShapeDtypeS...  113 us

profile of v3, /device:TPU:0, one launch (start us, length us, event | category | flops | bytes accessed | tf_op | source)
XLA Modules:
  0.0 269.8 jit_solution(2339552184420706584)
XLA Ops:
  0.6 1.0 pad_maximum_fusion
  1.7 0.8 copy.9
  2.4 112.7 %forward.1 = (bf16[4,2,2,4,2,3,8,1792]{7,6,5,4,3,2,1,0:T(8,128)(2,1)}, bf16[2,2,2,4,2,7,8,768]{7,6,5,4,3,2,1,0:T(8,128)(2,1)}, bf16[2048,768]{1,0:T(8,128)(2,1)}...) custom-call(bf16[2048,768]{1,0:T(8,128)(2,1)} %bitcast.19, ...), custom_call_target="tpu_custom_call" | custom-call | tf_op jit(solution)/shard_map/forward/pallas_call | solution.py:460
  115.1 148.4 %back.1 = (bf16[2048,768]{1,0:T(8,128)(2,1)}, bf16[4,3,8,1792]{3,2,1,0:T(8,128)(2,1)}, bf16[2,7,8,768]{3,2,1,0:T(8,128)(2,1)}, bf16[4,768,1792]{2,1,0:T(8,128)(2...) custom-call(bf16[2048,768]{1,0:T(8,128)(2,1)} %bitcast.23, bf16[2048,768]{1,0:T(8,128)(2,1)} %bitcast.20, ...), custom_call_target="tpu_custom_call" | custom-call | tf_op jit(solution)/shard_map/back/pallas_call | solution.py:697
  263.6 0.0 copy-start
  263.6 1.8 slice_bitcast_fusion
  265.4 3.8 %copy.16 = bf16[1,2048,768]{2,1,0:T(8,128)(2,1)} copy(bf16[1,2048,768]{2,1,0:T(8,128)(2,1)} %bitcast.24) | data formatting | bytes 6291456
  269.1 0.0 copy-done
  269.1 0.7 copy.17
Async XLA Ops:
  263.6 5.6 %copy-start = (bf16[2,7,8,768]{3,2,1,0:T(8,128)(2,1)S(1)}, bf16[2,7,8,768]{3,2,1,0:T(8,128)(2,1)}, u32[]{:S(2)}) copy-start(bf16[2,7,8,768]{3,2,1,0:T(8,128)(2,1)} %get-tuple-element.21) | copy-start | bytes 516100

commit v4 on v3

--- a/solution.py
+++ b/solution.py
@@ -343,9 +343,9 @@
     lax.fori_loop(0, number, one, 0)
 
 
-FORWARD_TIMES = ((0, 26), (12, 20), (22, 30), (44, 20))
-TILE_CLOCKS = ((27, 2.5), (58, 2.5))
-DOWN_CLOCK = (45, 2)
+FORWARD_TIMES = ((0, 22), (6, 22), (14, 40), (20, 55))
+TILE_CLOCKS = ((24, 4), (60, 4))
+DOWN_CLOCK = (52, 3)
 WIDE = 512
 
 
@@ -469,7 +469,7 @@
     )(x, gu_in, dn_in)
 
 
-BACK_TIMES = ((45, 26), (58, 16), (67, 24), (76, 16))
+BACK_TIMES = ((45, 34), (50, 30), (67, 30), (76, 26))
 GRADS_CLOCK = (46, 3)
 LATE_DOWN_CLOCK = (67, 1)
 LATE_STATES_CLOCK = (74, 2)

time: 270 us -> 252 us (0.933)
  Pallas kernels: 261 us -> 243 us
    pallas_call x1, Pallas kernels: 113 us -> 103 us  [forward(): pl.pallas_call(forward_kernel, name='forward', out_shape=(jax.ShapeDtypeS...]
    pallas_call x1, Pallas kernels: 148 us -> 140 us  [back(): pl.pallas_call(back_kernel, name='back', out_shape=(jax.ShapeDtypeStruct(...]
where the time goes in v4:
time: 252 us
  Pallas kernels  243 us (96%)
  local copies, waits for them, and re-layouts  6.97 us (3%)
    pallas_call x1, Pallas kernels, back(): pl.pallas_call(back_kernel, name='back', out_shape=(jax.ShapeDtypeStruct(...  140 us
    pallas_call x1, Pallas kernels, forward(): pl.pallas_call(forward_kernel, name='forward', out_shape=(jax.ShapeDtypeS...  103 us

profile of v4, /device:TPU:0, one launch (start us, length us, event | category | flops | bytes accessed | tf_op | source)
XLA Modules:
  0.0 251.7 jit_solution(10957785961824815275)
XLA Ops:
  0.6 1.0 pad_maximum_fusion
  1.7 0.8 copy.9
  2.4 102.7 %forward.1 = (bf16[4,2,2,4,2,3,8,1792]{7,6,5,4,3,2,1,0:T(8,128)(2,1)}, bf16[2,2,2,4,2,7,8,768]{7,6,5,4,3,2,1,0:T(8,128)(2,1)}, bf16[2048,768]{1,0:T(8,128)(2,1)}...) custom-call(bf16[2048,768]{1,0:T(8,128)(2,1)} %bitcast.19, ...), custom_call_target="tpu_custom_call" | custom-call | tf_op jit(solution)/shard_map/forward/pallas_call | solution.py:460
  105.1 140.3 %back.1 = (bf16[2048,768]{1,0:T(8,128)(2,1)}, bf16[4,3,8,1792]{3,2,1,0:T(8,128)(2,1)}, bf16[2,7,8,768]{3,2,1,0:T(8,128)(2,1)}, bf16[4,768,1792]{2,1,0:T(8,128)(2...) custom-call(bf16[2048,768]{1,0:T(8,128)(2,1)} %bitcast.23, bf16[2048,768]{1,0:T(8,128)(2,1)} %bitcast.20, ...), custom_call_target="tpu_custom_call" | custom-call | tf_op jit(solution)/shard_map/back/pallas_call | solution.py:697
  245.4 0.0 copy-start
  245.4 1.8 slice_bitcast_fusion
  247.2 3.8 %copy.16 = bf16[1,2048,768]{2,1,0:T(8,128)(2,1)} copy(bf16[1,2048,768]{2,1,0:T(8,128)(2,1)} %bitcast.24) | data formatting | bytes 6291456
  251.0 0.0 copy-done
  251.0 0.7 copy.17
Async XLA Ops:
  245.4 5.6 %copy-start = (bf16[2,7,8,768]{3,2,1,0:T(8,128)(2,1)S(1)}, bf16[2,7,8,768]{3,2,1,0:T(8,128)(2,1)}, u32[]{:S(2)}) copy-start(bf16[2,7,8,768]{3,2,1,0:T(8,128)(2,1)} %get-tuple-element.21) | copy-start | bytes 516100
